TPU v7x, 1024 devices: a whole 4x8x16 slice. The times are simulated.
1024 devices in a mesh: ctx: 32 (over z, core), exp: 32 (over y, x).
Axes of the slice: x: 4, y: 8, z: 16, core: 2. Of those that a mesh axis runs over, the one named last changes fastest.
Arguments:
- seq_inputs: bfloat16 [16384, 8192], P('ctx', 'exp'), may hold values from -6 to 6
- step_size: float32 [128, 16384], P('exp', 'ctx'), may hold values from 0.0007 to 0.14
- write_map: bfloat16 [16, 16384], P(None, 'ctx'), may hold values from -2 to 2
- read_map: bfloat16 [16, 16384], P(None, 'ctx'), may hold values from -2 to 2
- decay_log: float32 [128], P('exp'), may hold values from -9.3 to 1.4
- skip_gain: float32 [128], P('exp'), may hold values from 0.5 to 1.5
- moe_tokens: bfloat16 [4096, 4096], P('exp'), may hold values from -6 to 6
- expert_ids: int32 [4096, 2], P('exp'), may hold values from 0 to 15, all different within a row; in each aligned block of 128 rows (0 to 127, 128 to 255, ...) at most 32 rows name the same one
- route_weights: float32 [4096, 2], P('exp'), may hold values from 0.1 to 1
- gate_proj: bfloat16 [32, 4096, 3584], P('exp', None, 'ctx'), may hold values from -0.09375 to 0.09375
- up_proj: bfloat16 [32, 4096, 3584], P('exp', None, 'ctx'), may hold values from -0.09375 to 0.09375
- down_proj: bfloat16 [32, 3584, 4096], P('exp', None, 'ctx'), may hold values from -0.0625 to 0.0625
Outputs:
- mixer_output: bfloat16 [16384, 8192], P('ctx', 'exp')
- expert_output: bfloat16 [4096, 4096], P('exp', 'ctx')
Inputs may be any that keep to these rules, and one draw needn't show every extreme that they name: `expert_ids`: each row names two different experts. In the 128 rows of one index of exp (aligned blocks), no expert is named more than 32 times, and in some blocks an expert is named exactly 32 times.
All inputs are finite; a program needn't handle non-finite values.
Results may differ from a plain program's by a relative error of at most 0.002.
The roundings to bfloat16 on the way count: a program that leaves them out, or rounds other values in their place, can miss the bound.
Values may be sent and summed in bfloat16 or wider, within the bound.
No kernel may reach another device: no remote copies, remote signals or barrier semaphores. Data moves between devices by JAX's collectives and lax.ppermute only.
A program may use at most 64 MiB of HBM per device.

v0:
```python
import jax
import jax.numpy as jnp
from jax import lax
from jax.sharding import PartitionSpec as P

BLOCK = 256


HIGHEST = lax.Precision.HIGHEST


def side_by_side(arrays, axis, dim, along):
    columns = [a.reshape(*a.shape[:along], -1) for a in arrays]
    both = jnp.concatenate(columns, axis=along)
    result, at, done = (lax.all_gather(both, axis, axis=dim, tiled=True), 0, [])
    for a, column in zip(arrays, columns):
        section = result[..., at : at + column.shape[along]]
        done.append(section.reshape(*section.shape[:along], *a.shape[along:]))
        at += column.shape[along]
    return tuple(done)


def block_chain(running, pieces):
    decay, increment = pieces
    return (decay[:, None, None] * running + increment, running)


def mixer_prepare(seq_inputs, step_size, write_map, read_map, decay_log):
    length = seq_inputs.shape[0]
    head_count = step_size.shape[0]
    state_count = write_map.shape[0]
    head_width = seq_inputs.shape[1] // head_count
    block_count = length // BLOCK
    decay_rate = -jnp.exp(decay_log)
    log_decay = (step_size * decay_rate[:, None]).reshape(head_count, block_count, BLOCK)
    cumulative = jnp.cumsum(log_decay, axis=2)
    block_ends = cumulative[:, :, BLOCK - 1]
    step_blocks = step_size.reshape(head_count, block_count, BLOCK)
    write_blocks = write_map.reshape(state_count, block_count, BLOCK)
    read_blocks = read_map.reshape(state_count, block_count, BLOCK)
    value_blocks = seq_inputs.reshape(block_count, BLOCK, head_count, head_width)
    scores = jnp.einsum(
        "nkt,nks->kts", read_blocks, write_blocks, preferred_element_type=jnp.float32
    )
    row_index = lax.broadcasted_iota(jnp.int32, (BLOCK, BLOCK), 0)
    column_index = lax.broadcasted_iota(jnp.int32, (BLOCK, BLOCK), 1)
    lower = column_index <= row_index
    difference = cumulative[:, :, :, None] - cumulative[:, :, None, :]
    decay = jnp.where(lower[None, None], jnp.exp(jnp.minimum(difference, 0.0)), 0.0)
    mixing = (scores[None] * decay * step_blocks[:, :, None, :]).astype(jnp.bfloat16)
    local_mix = jnp.einsum(
        "hkts,kshp->kthp", mixing, value_blocks, preferred_element_type=jnp.float32
    )
    weights = jnp.exp(block_ends[:, :, None] - cumulative) * step_blocks
    key_decayed = (write_blocks[None] * weights[:, None]).astype(jnp.bfloat16)
    increments = jnp.einsum(
        "hnks,kshp->khnp", key_decayed, value_blocks, preferred_element_type=jnp.float32
    )
    zero_state = jnp.zeros((head_count, state_count, head_width), jnp.float32)
    final, entering = lax.scan(block_chain, zero_state, (jnp.exp(block_ends).T, increments))
    return (local_mix, cumulative, block_ends, entering, final)


def mixer_finish(
    local_mix, cumulative, block_ends, entering, state_before, read_map, seq_inputs, skip_gain
):
    head_count = block_ends.shape[0]
    block_count = block_ends.shape[1]
    state_count = read_map.shape[0]
    head_width = entering.shape[3]
    before = jnp.cumsum(block_ends, axis=1) - block_ends
    states = jnp.exp(before).T[:, :, None, None] * state_before[None] + entering
    read_blocks = read_map.reshape(state_count, block_count, BLOCK).astype(jnp.float32)
    carried = jnp.einsum("nkt,khnp->kthp", read_blocks, states, precision=HIGHEST)
    carried = carried * jnp.exp(cumulative).transpose(1, 2, 0)[:, :, :, None]
    value_blocks = seq_inputs.reshape(block_count, BLOCK, head_count, head_width).astype(
        jnp.float32
    )
    output = local_mix + carried + skip_gain[None, None, :, None] * value_blocks
    return output.reshape(seq_inputs.shape).astype(jnp.bfloat16)


CTX = ("zh", "zl", "core")
SWAP = ((0, 1), (1, 0))
CHUNKS = 1


def swap(array, axis):
    return lax.ppermute(array, axis, SWAP)


def four(array, across):
    beside = swap(array, "core")
    return (array, beside, across, swap(across, "core"))


def ring(array):
    count = lax.axis_size("zh")
    rows = array.shape[0]
    ahead = [(i, (i + 1) % count) for i in range(count)]
    behind = [(i, (i - 1) % count) for i in range(count)]
    yield 0, 0, array
    forward, backward = array, array
    for step in range(1, count // 2):
        forward = lax.ppermute(forward, "zh", ahead)
        backward = lax.ppermute(backward, "zh", behind)
        yield -step, 0, forward
        yield step, 0, backward
    half = rows // 2
    yield -(count // 2), 0, lax.ppermute(forward[:half], "zh", ahead)
    yield count // 2, half, lax.ppermute(backward[half:], "zh", behind)


def absolute(pieces):
    zl = lax.axis_index("zl")
    core = lax.axis_index("core")
    first, second, third, fourth = pieces
    low = jnp.where(core == 0, first, second), jnp.where(core == 0, second, first)
    high = jnp.where(core == 0, third, fourth), jnp.where(core == 0, fourth, third)
    low = jnp.stack(low)
    high = jnp.stack(high)
    return jnp.concatenate(
        [jnp.where(zl == 0, low, high), jnp.where(zl == 0, high, low)], axis=0
    )


def joined(first, second):
    return first[0] + second[0], jnp.exp(second[0])[:, None, None] * first[1] + second[1]


def exchanged(pair, axis):
    log, state = pair
    both = jnp.concatenate([log[:, None], state.reshape(state.shape[0], -1)], axis=1)
    received = swap(both, axis)
    return received[:, 0], received[:, 1:].reshape(state.shape)


def chosen(flag, left, right):
    return jax.tree.map(lambda a, b: jnp.where(flag, a, b), left, right)


def carry(total_log, final):
    own = (total_log, final)
    before = jax.tree.map(jnp.zeros_like, own)
    for axis in ("core", "zl"):
        other = exchanged(own, axis)
        later = lax.axis_index(axis) == 1
        before = chosen(later, joined(other, before), before)
        own = chosen(later, joined(other, own), joined(own, other))
    logs, states = side_by_side((own[0][None], own[1][None]), "zh", 0, 2)
    count = lax.axis_size("zh")
    place = lax.axis_index("zh")
    source = lax.broadcasted_iota(jnp.int32, (count, count), 0)
    target = lax.broadcasted_iota(jnp.int32, (count, count), 1)
    between = ((target > source) & (target < place)).astype(jnp.float32)
    log_span = jnp.dot(between, logs, precision=HIGHEST, preferred_element_type=jnp.float32)
    earlier = lax.broadcasted_iota(jnp.int32, (count, 1), 0) < place
    factor = jnp.where(earlier, jnp.exp(log_span), 0.0)
    outside = jnp.sum(factor[:, :, None, None] * states, axis=0)
    return joined((jnp.zeros_like(total_log), outside), before)[1]


def route(expert_ids, route_weights, expert_count, rows):
    group_size = expert_ids.shape[0]
    quarter = CHUNKS * rows
    part = lax.axis_index("zl") * 2 + lax.axis_index("core")
    assigned = expert_ids.reshape(group_size * 2)
    onehot = (
        assigned[:, None] == lax.broadcasted_iota(jnp.int32, (group_size * 2, expert_count), 1)
    ).astype(jnp.int32)
    earlier_count = jnp.cumsum(onehot, axis=0) - onehot
    slot = jnp.sum(earlier_count * onehot, axis=1) - part * quarter
    position = jnp.where((slot >= 0) & (slot < quarter), assigned * quarter + slot, -1)
    matches = (
        position[:, None]
        == lax.broadcasted_iota(jnp.int32, (group_size * 2, expert_count * quarter), 1)
    ).astype(jnp.float32)
    shape = (group_size, 2, expert_count, CHUNKS, rows)
    dispatch = jnp.sum(matches.reshape(shape), axis=1).astype(jnp.bfloat16)
    combine = jnp.sum(
        (matches * route_weights.reshape(group_size * 2)[:, None]).reshape(shape), axis=1
    )
    return dispatch, combine


def exchange(array):
    return lax.all_to_all(array, "exp", split_axis=0, concat_axis=0, tiled=True)


def send_slots(moe_tokens, dispatch):
    group_size, expert_count, _, rows = dispatch.shape
    packed = []
    for chunk in range(CHUNKS):
        onehot = jnp.broadcast_to(
            dispatch[:, :, chunk, :][:, :, None, :], (group_size, expert_count, 2, rows)
        )
        packed.append(
            jnp.einsum(
                "iehs,id->ehsd", onehot, moe_tokens, preferred_element_type=jnp.float32
            )
            .astype(jnp.bfloat16)
            .reshape(2 * expert_count, rows, -1)
        )
    return packed


def hidden_units(arrived, weights, hidden_count):
    pieces = []
    for weight in weights:
        sums = lax.dot_general(
            weight, arrived, (((0,), (1,)), ((), ())), preferred_element_type=jnp.float32
        ).reshape(2, 2, hidden_count, -1)
        acted = (jax.nn.silu(sums[:, 0]) * sums[:, 1]).astype(jnp.bfloat16)
        pieces.extend((acted[0], acted[1]))
    return absolute(pieces).reshape(4 * hidden_count, -1)


def down_sums(hidden, down):
    place = lax.axis_index("zh")
    count = lax.axis_size("zh")
    size = hidden.shape[0]
    total = 0.0
    for offset, first, shard in ring(hidden):
        start = (place + (offset + count)) % count * size + first
        rows = lax.dynamic_slice_in_dim(down, start, shard.shape[0], 0)
        total = total + lax.dot_general(
            shard, rows, (((0,), (0,)), ((), ())), preferred_element_type=jnp.float32
        )
    return total


def combined(returned, combine):
    group_size, expert_count, rows = combine.shape
    summed = jnp.sum(returned.reshape(expert_count, 2, rows, -1), axis=1)
    return jnp.dot(
        combine.reshape(group_size, expert_count * rows),
        summed.reshape(expert_count * rows, -1),
        precision=HIGHEST,
        preferred_element_type=jnp.float32,
    )


def shared_out(result):
    width = result.shape[1] // 4
    total = result[:, :width]
    for r in (3, 2, 1):
        total = total + lax.ppermute(
            result[:, r * width : (r + 1) * width], ("zl", "core"), [(i, i ^ r) for i in range(4)]
        )
    return total.astype(jnp.bfloat16)


def layer(
    seq_inputs,
    step_size,
    write_map,
    read_map,
    decay_log,
    skip_gain,
    moe_tokens,
    expert_ids,
    route_weights,
    gate_proj,
    up_proj,
    down_proj,
):
    expert_count = lax.axis_size("exp") // 2
    rows = min(moe_tokens.shape[0], 4 * moe_tokens.shape[0] // expert_count) // 4 // CHUNKS
    hidden_count = gate_proj.shape[2]
    gate, up, down = gate_proj[0], up_proj[0], down_proj[0]
    gate_across = swap(gate, "zl")
    up_across = swap(up, "zl")
    dispatch, combine = route(expert_ids, route_weights, expert_count, rows)
    packed = send_slots(moe_tokens, dispatch)
    packed, gate, up, down, seq_inputs, step_size = lax.optimization_barrier(
        (packed, gate, up, down, seq_inputs, step_size)
    )
    arrived = [exchange(chunk) for chunk in packed]
    down_across = swap(down, "zl")
    gates = four(gate, gate_across)
    ups = four(up, up_across)
    weights = [
        jnp.concatenate([gates[r], ups[r], gates[r + 1], ups[r + 1]], axis=1) for r in (0, 2)
    ]
    down_columns = jnp.concatenate(four(down, down_across), axis=1)
    local_mix, cumulative, block_ends, entering, final = mixer_prepare(
        seq_inputs, step_size, write_map, read_map, decay_log
    )
    sums = [
        down_sums(
            hidden_units(a.reshape(2 * expert_count * rows, -1), weights, hidden_count),
            down_columns,
        )
        for a in arrived
    ]
    total_log = jnp.sum(block_ends, axis=1)
    returned = [exchange(part.reshape(2 * expert_count, rows, -1)) for part in sums]
    state_before = carry(total_log, final)
    mixer_output = mixer_finish(
        local_mix, cumulative, block_ends, entering, state_before, read_map, seq_inputs, skip_gain
    )
    result = sum(combined(part, combine[:, :, chunk]) for chunk, part in enumerate(returned))
    expert_output = shared_out(result)
    return (mixer_output, expert_output)


def solution(mesh):
    devices = mesh.devices
    ctx_size, exp_size = devices.shape
    split = jax.sharding.Mesh(
        devices.reshape(ctx_size // 4, 2, 2, exp_size), ("zh", "zl", "core", "exp")
    )
    return jax.shard_map(
        layer,
        mesh=split,
        in_specs=(
            P(CTX, "exp"),
            P("exp", CTX),
            P(None, CTX),
            P(None, CTX),
            P("exp"),
            P("exp"),
            P("exp", None),
            P("exp", None),
            P("exp", None),
            P("exp", None, CTX),
            P("exp", None, CTX),
            P("exp", None, CTX),
        ),
        out_specs=(P(CTX, "exp"), P("exp", CTX)),
        check_vma=False,
    )
```

profile of v0, /device:TPU:1, one launch (start us, length us, event | category | flops | bytes accessed | tf_op | source)
XLA Modules:
  0.0 234.1 jit_solution(6991061802026554255)
XLA Ops:
  0.6 5.0 %collective-permute-start.4 = (bf16[4096,112]{0,1:T(8,128)(2,1)}, bf16[4096,112]{0,1:T(8,128)(2,1)}, u32[]{:S(2)}, u32[]{:S(2)}) collective-permute-start(bf16[4096,112]{0,1:T(8,128)(2,1)} %bitcast.163), channel_id=1, source_target_pairs={{0,64},{64,0},{1,65},{65,1},{2,66},{66,2},{3,67},{67,3},{4,68},{68... | collective-permute-start | bytes 2752520 | tf_op jit(solution)/shard_map/ppermute | solution.py:89
  13.4 15.2 %collective-permute-start.8 = (bf16[3584,128]{1,0:T(8,128)(2,1)}, bf16[3584,128]{1,0:T(8,128)(2,1)}, u32[]{:S(2)}, u32[]{:S(2)}) collective-permute-start(bf16[3584,128]{1,0:T(8,128)(2,1)} %bitcast.6), channel_id=1, source_target_pairs={{0,32},{32,0},{1,33},{33,1},{2,34},{34,2},{3,35},{35,3},{4,36},{36... | collective-permute-start | bytes 2752520 | tf_op jit(solution)/shard_map/ppermute | solution.py:89
  30.6 4.8 %all-to-all-start = ((bf16[32,8,4096]{2,1,0:T(8,128)(2,1)}), bf16[32,8,4096]{2,1,0:T(8,128)(2,1)}, u32[]{:S(2)}, u32[]{:S(2)}) async-start(bf16[32,8,4096]{2,1,0:T(8,128)(2,1)} %bitcast.3), calls=%async_computation | async-start | bytes 4194304 | tf_op jit(solution)/shard_map/all_to_all | solution.py:187
  35.5 2.4 %reduce-window.16 = f32[4,2,2,128]{3,2,1,0:T(2,128)S(1)} reduce-window(f32[4,2,2,128]{3,2,1,0:T(2,128)S(1)} %reshape.302, f32[]{:T(128)} %constant.114.clone.1), window={size=1x1x1x128 pad=0_0x0_0x0_0x127_0}, to_apply=%region_4.5 | reduce-window | flops 260096 | bytes 16388 | tf_op jit(solution)/shard_map/reduce-window.2
  47.8 3.6 %collective-permute-start.1 = (f32[4,1025]{1,0:T(4,128)S(1)}, f32[4,1025]{1,0:T(4,128)S(1)}, u32[]{:S(2)}, u32[]{:S(2)}) collective-permute-start(f32[4,1025]{1,0:T(4,128)S(1)} %pad_maximum_fusion.6), channel_id=1, source_target_pairs={{0,64},{64,0},{1,65},{65,1},{2,66},{66,2},{3,67},{67,3},{4,68},{68... | collective-permute-start | bytes 49208 | tf_op jit(solution)/shard_map/ppermute | solution.py:89
  51.7 3.2 %collective-permute-done.1 = f32[4,1025]{1,0:T(4,128)S(1)} collective-permute-done((f32[4,1025]{1,0:T(4,128)S(1)}, f32[4,1025]{1,0:T(4,128)S(1)}, u32[]{:S(2)}, u32[]{:S(2)}) %collective-permute-start.1) | collective-permute-done | bytes 16432 | tf_op jit(solution)/shard_map/ppermute | solution.py:89
  54.9 13.8 %collective-permute-start.2 = (bf16[4096,112]{0,1:T(8,128)(2,1)S(1)}, bf16[4096,112]{0,1:T(8,128)(2,1)}, u32[]{:S(2)}, u32[]{:S(2)}) collective-permute-start(bf16[4096,112]{0,1:T(8,128)(2,1)S(1)} %bitcast.164), channel_id=1, source_target_pairs={{0,32},{32,0},{1,33},{33,1},{2,34},{34,2},{3,35},{35,3},{4,36},{36... | collective-permute-start | bytes 2752520 | tf_op jit(solution)/shard_map/ppermute | solution.py:89
  73.2 2.4 %collective-permute-start.6 = (bf16[4096,112]{0,1:T(8,128)(2,1)}, bf16[4096,112]{0,1:T(8,128)(2,1)S(1)}, u32[]{:S(2)}, u32[]{:S(2)}) collective-permute-start(bf16[4096,112]{0,1:T(8,128)(2,1)} %collective-permute-done.4), channel_id=1, source_target_pairs={{0,32},{32,0},{1,33},{33,1},{2,34},{34,2},{3,35},{35,3},{4,36},{36... | collective-permute-start | bytes 2752520 | tf_op jit(solution)/shard_map/ppermute | solution.py:89
  77.5 2.4 %collective-permute-start.10 = (bf16[3584,128]{1,0:T(8,128)(2,1)}, bf16[3584,128]{1,0:T(8,128)(2,1)}, u32[]{:S(2)}, u32[]{:S(2)}) collective-permute-start(bf16[3584,128]{1,0:T(8,128)(2,1)} %collective-permute-done.9), channel_id=1, source_target_pairs={{0,32},{32,0},{1,33},{33,1},{2,34},{34,2},{3,35},{35,3},{4,36},{36... | collective-permute-start | bytes 2752520 | tf_op jit(solution)/shard_map/ppermute | solution.py:89
  84.4 5.5 %pad_maximum_fusion = bf16[4096,448]{0,1:T(8,128)(2,1)} fusion(bf16[4096,112]{0,1:T(8,128)(2,1)S(1)} %collective-permute-done.3, bf16[4096,112]{0,1:T(8,128)(2,1)} %collective-permute-done.2, bf16[4096,112]{0,1:T(8,128)(2,1)S(1)} %bitcast.162, bf16[4096,112]{0,1:T(8,128)(2,1)S(1)} %bitcast.165), kind=kLoop, calls=%fused_computation.5 | loop fusion | flops 14680064 | bytes 7340032 | tf_op jit(solution)/shard_map/concatenate | solution.py:283
  89.8 3.2 %pad_maximum_fusion.1 = bf16[4096,448]{0,1:T(8,128)(2,1)} fusion(bf16[4096,112]{0,1:T(8,128)(2,1)S(1)} %collective-permute-done.7, bf16[4096,112]{0,1:T(8,128)(2,1)S(1)} %collective-permute-done.6, bf16[4096,112]{0,1:T(8,128)(2,1)} %collective-permute-done.5, bf16[4096,112]{0,1:T(8,128)(2,1)} %collective-permute-done.4), kind=kLoop, calls=%fused_computation.6 | loop fusion | flops 14680064 | bytes 7340032 | tf_op jit(solution)/shard_map/concatenate | solution.py:283
  93.1 4.0 %fusion.3 = f32[2,2,112,256]{3,2,1,0:T(8,128)S(1)} fusion(bf16[2,2,112,4096]{3,2,1,0:T(8,128)(2,1)} %bitcast.154, bf16[32,8,4096]{2,1,0:T(8,128)(2,1)} %all-to-all-done), kind=kOutput, calls=%fused_computation.9 | convolution fusion | flops 939524096 | bytes 6225920 | tf_op jit(solution)/shard_map/dot_general | solution.py:210
  97.1 3.0 %fusion.1 = f32[2,2,112,256]{3,2,0,1:T(8,128)S(1)} fusion(bf16[2,2,112,4096]{3,2,1,0:T(8,128)(2,1)S(1)} %bitcast.155, bf16[32,8,4096]{2,1,0:T(8,128)(2,1)} %all-to-all-done), kind=kOutput, calls=%fused_computation.7 | convolution fusion | flops 939524096 | bytes 6225920 | tf_op jit(solution)/shard_map/dot_general | solution.py:210
  100.4 5.8 %collective-permute-start.11 = (bf16[448,256]{1,0:T(8,128)(2,1)S(1)}, bf16[448,256]{1,0:T(8,128)(2,1)S(1)}, u32[]{:S(2)}, u32[]{:S(2)}) collective-permute-start(bf16[448,256]{1,0:T(8,128)(2,1)S(1)} %bitcast.157), channel_id=1, source_target_pairs={{0,128},{128,256},{256,384},{384,512},{512,640},{640,768},{768,896... | collective-permute-start | bytes 688136 | tf_op jit(solution)/shard_map/ppermute | solution.py:105
  106.2 13.4 %collective-permute-start.12 = (bf16[448,256]{1,0:T(8,128)(2,1)S(1)}, bf16[448,256]{1,0:T(8,128)(2,1)S(1)}, u32[]{:S(2)}, u32[]{:S(2)}) collective-permute-start(bf16[448,256]{1,0:T(8,128)(2,1)S(1)} %bitcast.158), channel_id=1, source_target_pairs={{0,896},{128,0},{256,128},{384,256},{512,384},{640,512},{768,640},... | collective-permute-start | bytes 688136 | tf_op jit(solution)/shard_map/ppermute | solution.py:106
  121.0 8.3 %collective-permute-done.12 = bf16[448,256]{1,0:T(8,128)(2,1)S(1)} collective-permute-done((bf16[448,256]{1,0:T(8,128)(2,1)S(1)}, bf16[448,256]{1,0:T(8,128)(2,1)S(1)}, u32[]{:S(2)}, u32[]{:S(2)}) %collective-permute-start.12) | collective-permute-done | bytes 229408 | tf_op jit(solution)/shard_map/ppermute | solution.py:106
  129.3 6.3 %collective-permute-start.14 = (bf16[448,256]{1,0:T(8,128)(2,1)S(1)}, bf16[448,256]{1,0:T(8,128)(2,1)S(1)}, u32[]{:S(2)}, u32[]{:S(2)}) collective-permute-start(bf16[448,256]{1,0:T(8,128)(2,1)S(1)} %collective-permute-done.12), channel_id=1, source_target_pairs={{0,896},{128,0},{256,128},{384,256},{512,384},{640,512},{768,640},... | collective-permute-start | bytes 688136 | tf_op jit(solution)/shard_map/ppermute | solution.py:106
  139.7 11.1 %collective-permute-start.16 = (bf16[448,256]{1,0:T(8,128)(2,1)S(1)}, bf16[448,256]{1,0:T(8,128)(2,1)S(1)}, u32[]{:S(2)}, u32[]{:S(2)}) collective-permute-start(bf16[448,256]{1,0:T(8,128)(2,1)S(1)} %collective-permute-done.14), channel_id=1, source_target_pairs={{0,896},{128,0},{256,128},{384,256},{512,384},{640,512},{768,640},... | collective-permute-start | bytes 688136 | tf_op jit(solution)/shard_map/ppermute | solution.py:106
  153.4 8.9 %collective-permute-done.15 = bf16[448,256]{1,0:T(8,128)(2,1)S(1)} collective-permute-done((bf16[448,256]{1,0:T(8,128)(2,1)S(1)}, bf16[448,256]{1,0:T(8,128)(2,1)S(1)}, u32[]{:S(2)}, u32[]{:S(2)}) %collective-permute-start.15) | collective-permute-done | bytes 229408 | tf_op jit(solution)/shard_map/ppermute | solution.py:105
  164.2 5.7 %collective-permute-start.18 = (bf16[224,256]{1,0:T(8,128)(2,1)S(1)}, bf16[224,256]{1,0:T(8,128)(2,1)S(1)}, u32[]{:S(2)}, u32[]{:S(2)}) collective-permute-start(bf16[224,256]{1,0:T(8,128)(2,1)S(1)} %slice.119), channel_id=1, source_target_pairs={{0,896},{128,0},{256,128},{384,256},{512,384},{640,512},{768,640},... | collective-permute-start | bytes 344072 | tf_op jit(solution)/shard_map/ppermute | solution.py:111
  172.9 9.4 %all-to-all-start.1 = ((f32[32,8,512]{2,1,0:T(8,128)}), f32[32,8,512]{2,1,0:T(8,128)S(1)}, u32[]{:S(2)}, u32[]{:S(2)}) async-start(f32[32,8,512]{2,1,0:T(8,128)} %fusion.12), calls=%async_computation.1 | async-start | bytes 1048576 | tf_op jit(solution)/shard_map/all_to_all | solution.py:187
  182.4 22.8 %all_gather.3 = f32[8,4,1025]{2,1,0:T(4,128)S(1)} all-gather(f32[1,4,1025]{2,1,0:T(4,128)S(1)} %pad_maximum_fusion.7), channel_id=1, replica_groups=mesh['zh'=8,'zl'=2,'core'=2,'exp'=32] {'zh'}, dimensions={0}, use_global_device_ids=true | all-gather | bytes 147600 | tf_op jit(solution)/shard_map/all_gather | solution.py:15
  208.8 15.6 %collective-permute-start.19 = (f32[128,128]{1,0:T(8,128)}, f32[128,128]{1,0:T(8,128)S(1)}, u32[]{:S(2)}, u32[]{:S(2)}) collective-permute-start(f32[128,128]{1,0:T(8,128)} %get-tuple-element.82), channel_id=1, source_target_pairs={{0,96},{32,64},{64,32},{96,0},{1,97},{33,65},{65,33},{97,1},{2,98}... | collective-permute-start | bytes 196616 | tf_op jit(solution)/shard_map/ppermute | solution.py:247
  224.4 3.3 %collective-permute-start.20 = (f32[128,128]{1,0:T(8,128)}, f32[128,128]{1,0:T(8,128)}, u32[]{:S(2)}, u32[]{:S(2)}) collective-permute-start(f32[128,128]{1,0:T(8,128)} %get-tuple-element.84), channel_id=1, source_target_pairs={{0,64},{32,96},{64,0},{96,32},{1,65},{33,97},{65,1},{97,33},{2,66}... | collective-permute-start | bytes 196616 | tf_op jit(solution)/shard_map/ppermute | solution.py:247
  (174 shorter events, 53.6 us)
Async XLA Ops:
  0.6 70.6 %collective-permute-start.4 = (bf16[4096,112]{0,1:T(8,128)(2,1)}, bf16[4096,112]{0,1:T(8,128)(2,1)}, u32[]{:S(2)}, u32[]{:S(2)}) collective-permute-start(bf16[4096,112]{0,1:T(8,128)(2,1)} %bitcast.163), channel_id=1, source_target_pairs={{0,64},{64,0},{1,65},{65,1},{2,66},{66,2},{3,67},{67,3},{4,68},{68... | collective-permute-start | bytes 2752520 | tf_op jit(solution)/shard_map/ppermute | solution.py:89
  5.6 67.5 %collective-permute-start.5 = (bf16[4096,112]{0,1:T(8,128)(2,1)}, bf16[4096,112]{0,1:T(8,128)(2,1)}, u32[]{:S(2)}, u32[]{:S(2)}) collective-permute-start(bf16[4096,112]{0,1:T(8,128)(2,1)} %bitcast.160), channel_id=1, source_target_pairs={{0,64},{64,0},{1,65},{65,1},{2,66},{66,2},{3,67},{67,3},{4,68},{68... | collective-permute-start | bytes 2752520 | tf_op jit(solution)/shard_map/ppermute | solution.py:89
  13.4 62.1 %collective-permute-start.8 = (bf16[3584,128]{1,0:T(8,128)(2,1)}, bf16[3584,128]{1,0:T(8,128)(2,1)}, u32[]{:S(2)}, u32[]{:S(2)}) collective-permute-start(bf16[3584,128]{1,0:T(8,128)(2,1)} %bitcast.6), channel_id=1, source_target_pairs={{0,32},{32,0},{1,33},{33,1},{2,34},{34,2},{3,35},{35,3},{4,36},{36... | collective-permute-start | bytes 2752520 | tf_op jit(solution)/shard_map/ppermute | solution.py:89
  28.7 48.8 %collective-permute-start.9 = (bf16[3584,128]{1,0:T(8,128)(2,1)}, bf16[3584,128]{1,0:T(8,128)(2,1)}, u32[]{:S(2)}, u32[]{:S(2)}) collective-permute-start(bf16[3584,128]{1,0:T(8,128)(2,1)} %bitcast.6), channel_id=1, source_target_pairs={{0,64},{64,0},{1,65},{65,1},{2,66},{66,2},{3,67},{67,3},{4,68},{68... | collective-permute-start | bytes 2752520 | tf_op jit(solution)/shard_map/ppermute | solution.py:89
  30.6 62.5 %all-to-all-start = ((bf16[32,8,4096]{2,1,0:T(8,128)(2,1)}), bf16[32,8,4096]{2,1,0:T(8,128)(2,1)}, u32[]{:S(2)}, u32[]{:S(2)}) async-start(bf16[32,8,4096]{2,1,0:T(8,128)(2,1)} %bitcast.3), calls=%async_computation | async-start | bytes 4194304 | tf_op jit(solution)/shard_map/all_to_all | solution.py:187
  40.7 6.5 %collective-permute-start = (f32[4,1025]{1,0:T(4,128)S(1)}, f32[4,1025]{1,0:T(4,128)S(1)}, u32[]{:S(2)}, u32[]{:S(2)}) collective-permute-start(f32[4,1025]{1,0:T(4,128)S(1)} %pad_maximum_fusion.5), channel_id=1, source_target_pairs={{0,32},{32,0},{1,33},{33,1},{2,34},{34,2},{3,35},{35,3},{4,36},{36... | collective-permute-start | bytes 49208 | tf_op jit(solution)/shard_map/ppermute | solution.py:89
  47.8 7.1 %collective-permute-start.1 = (f32[4,1025]{1,0:T(4,128)S(1)}, f32[4,1025]{1,0:T(4,128)S(1)}, u32[]{:S(2)}, u32[]{:S(2)}) collective-permute-start(f32[4,1025]{1,0:T(4,128)S(1)} %pad_maximum_fusion.6), channel_id=1, source_target_pairs={{0,64},{64,0},{1,65},{65,1},{2,66},{66,2},{3,67},{67,3},{4,68},{68... | collective-permute-start | bytes 49208 | tf_op jit(solution)/shard_map/ppermute | solution.py:89
  54.9 29.5 %collective-permute-start.2 = (bf16[4096,112]{0,1:T(8,128)(2,1)S(1)}, bf16[4096,112]{0,1:T(8,128)(2,1)}, u32[]{:S(2)}, u32[]{:S(2)}) collective-permute-start(bf16[4096,112]{0,1:T(8,128)(2,1)S(1)} %bitcast.164), channel_id=1, source_target_pairs={{0,32},{32,0},{1,33},{33,1},{2,34},{34,2},{3,35},{35,3},{4,36},{36... | collective-permute-start | bytes 2752520 | tf_op jit(solution)/shard_map/ppermute | solution.py:89
  71.2 13.2 %collective-permute-start.3 = (bf16[4096,112]{0,1:T(8,128)(2,1)S(1)}, bf16[4096,112]{0,1:T(8,128)(2,1)S(1)}, u32[]{:S(2)}, u32[]{:S(2)}) collective-permute-start(bf16[4096,112]{0,1:T(8,128)(2,1)S(1)} %bitcast.161), channel_id=1, source_target_pairs={{0,32},{32,0},{1,33},{33,1},{2,34},{34,2},{3,35},{35,3},{4,36},{36... | collective-permute-start | bytes 2752520 | tf_op jit(solution)/shard_map/ppermute | solution.py:89
  73.2 16.7 %collective-permute-start.6 = (bf16[4096,112]{0,1:T(8,128)(2,1)}, bf16[4096,112]{0,1:T(8,128)(2,1)S(1)}, u32[]{:S(2)}, u32[]{:S(2)}) collective-permute-start(bf16[4096,112]{0,1:T(8,128)(2,1)} %collective-permute-done.4), channel_id=1, source_target_pairs={{0,32},{32,0},{1,33},{33,1},{2,34},{34,2},{3,35},{35,3},{4,36},{36... | collective-permute-start | bytes 2752520 | tf_op jit(solution)/shard_map/ppermute | solution.py:89
  75.6 14.3 %collective-permute-start.7 = (bf16[4096,112]{0,1:T(8,128)(2,1)}, bf16[4096,112]{0,1:T(8,128)(2,1)S(1)}, u32[]{:S(2)}, u32[]{:S(2)}) collective-permute-start(bf16[4096,112]{0,1:T(8,128)(2,1)} %collective-permute-done.5), channel_id=1, source_target_pairs={{0,32},{32,0},{1,33},{33,1},{2,34},{34,2},{3,35},{35,3},{4,36},{36... | collective-permute-start | bytes 2752520 | tf_op jit(solution)/shard_map/ppermute | solution.py:89
  77.5 42.1 %collective-permute-start.10 = (bf16[3584,128]{1,0:T(8,128)(2,1)}, bf16[3584,128]{1,0:T(8,128)(2,1)}, u32[]{:S(2)}, u32[]{:S(2)}) collective-permute-start(bf16[3584,128]{1,0:T(8,128)(2,1)} %collective-permute-done.9), channel_id=1, source_target_pairs={{0,32},{32,0},{1,33},{33,1},{2,34},{34,2},{3,35},{35,3},{4,36},{36... | collective-permute-start | bytes 2752520 | tf_op jit(solution)/shard_map/ppermute | solution.py:89
  100.4 35.3 %collective-permute-start.11 = (bf16[448,256]{1,0:T(8,128)(2,1)S(1)}, bf16[448,256]{1,0:T(8,128)(2,1)S(1)}, u32[]{:S(2)}, u32[]{:S(2)}) collective-permute-start(bf16[448,256]{1,0:T(8,128)(2,1)S(1)} %bitcast.157), channel_id=1, source_target_pairs={{0,128},{128,256},{256,384},{384,512},{512,640},{640,768},{768,896... | collective-permute-start | bytes 688136 | tf_op jit(solution)/shard_map/ppermute | solution.py:105
  106.2 23.1 %collective-permute-start.12 = (bf16[448,256]{1,0:T(8,128)(2,1)S(1)}, bf16[448,256]{1,0:T(8,128)(2,1)S(1)}, u32[]{:S(2)}, u32[]{:S(2)}) collective-permute-start(bf16[448,256]{1,0:T(8,128)(2,1)S(1)} %bitcast.158), channel_id=1, source_target_pairs={{0,896},{128,0},{256,128},{384,256},{512,384},{640,512},{768,640},... | collective-permute-start | bytes 688136 | tf_op jit(solution)/shard_map/ppermute | solution.py:106
  129.3 10.3 %collective-permute-start.14 = (bf16[448,256]{1,0:T(8,128)(2,1)S(1)}, bf16[448,256]{1,0:T(8,128)(2,1)S(1)}, u32[]{:S(2)}, u32[]{:S(2)}) collective-permute-start(bf16[448,256]{1,0:T(8,128)(2,1)S(1)} %collective-permute-done.12), channel_id=1, source_target_pairs={{0,896},{128,0},{256,128},{384,256},{512,384},{640,512},{768,640},... | collective-permute-start | bytes 688136 | tf_op jit(solution)/shard_map/ppermute | solution.py:106
  135.7 15.4 %collective-permute-start.13 = (bf16[448,256]{1,0:T(8,128)(2,1)S(1)}, bf16[448,256]{1,0:T(8,128)(2,1)S(1)}, u32[]{:S(2)}, u32[]{:S(2)}) collective-permute-start(bf16[448,256]{1,0:T(8,128)(2,1)S(1)} %collective-permute-done.11), channel_id=1, source_target_pairs={{0,128},{128,256},{256,384},{384,512},{512,640},{640,768},{768,896... | collective-permute-start | bytes 688136 | tf_op jit(solution)/shard_map/ppermute | solution.py:105
  139.7 24.5 %collective-permute-start.16 = (bf16[448,256]{1,0:T(8,128)(2,1)S(1)}, bf16[448,256]{1,0:T(8,128)(2,1)S(1)}, u32[]{:S(2)}, u32[]{:S(2)}) collective-permute-start(bf16[448,256]{1,0:T(8,128)(2,1)S(1)} %collective-permute-done.14), channel_id=1, source_target_pairs={{0,896},{128,0},{256,128},{384,256},{512,384},{640,512},{768,640},... | collective-permute-start | bytes 688136 | tf_op jit(solution)/shard_map/ppermute | solution.py:106
  151.1 11.1 %collective-permute-start.15 = (bf16[448,256]{1,0:T(8,128)(2,1)S(1)}, bf16[448,256]{1,0:T(8,128)(2,1)S(1)}, u32[]{:S(2)}, u32[]{:S(2)}) collective-permute-start(bf16[448,256]{1,0:T(8,128)(2,1)S(1)} %collective-permute-done.13), channel_id=1, source_target_pairs={{0,128},{128,256},{256,384},{384,512},{512,640},{640,768},{768,896... | collective-permute-start | bytes 688136 | tf_op jit(solution)/shard_map/ppermute | solution.py:105
  162.3 8.0 %collective-permute-start.17 = (bf16[224,256]{1,0:T(8,128)(2,1)S(1)}, bf16[224,256]{1,0:T(8,128)(2,1)S(1)}, u32[]{:S(2)}, u32[]{:S(2)}) collective-permute-start(bf16[224,256]{1,0:T(8,128)(2,1)S(1)} %slice.118), channel_id=1, source_target_pairs={{0,128},{128,256},{256,384},{384,512},{512,640},{640,768},{768,896... | collective-permute-start | bytes 344072 | tf_op jit(solution)/shard_map/ppermute | solution.py:110
  164.2 7.3 %collective-permute-start.18 = (bf16[224,256]{1,0:T(8,128)(2,1)S(1)}, bf16[224,256]{1,0:T(8,128)(2,1)S(1)}, u32[]{:S(2)}, u32[]{:S(2)}) collective-permute-start(bf16[224,256]{1,0:T(8,128)(2,1)S(1)} %slice.119), channel_id=1, source_target_pairs={{0,896},{128,0},{256,128},{384,256},{512,384},{640,512},{768,640},... | collective-permute-start | bytes 344072 | tf_op jit(solution)/shard_map/ppermute | solution.py:111
  172.9 34.8 %all-to-all-start.1 = ((f32[32,8,512]{2,1,0:T(8,128)}), f32[32,8,512]{2,1,0:T(8,128)S(1)}, u32[]{:S(2)}, u32[]{:S(2)}) async-start(f32[32,8,512]{2,1,0:T(8,128)} %fusion.12), calls=%async_computation.1 | async-start | bytes 1048576 | tf_op jit(solution)/shard_map/all_to_all | solution.py:187
  208.8 23.8 %collective-permute-start.19 = (f32[128,128]{1,0:T(8,128)}, f32[128,128]{1,0:T(8,128)S(1)}, u32[]{:S(2)}, u32[]{:S(2)}) collective-permute-start(f32[128,128]{1,0:T(8,128)} %get-tuple-element.82), channel_id=1, source_target_pairs={{0,96},{32,64},{64,32},{96,0},{1,97},{33,65},{65,33},{97,1},{2,98}... | collective-permute-start | bytes 196616 | tf_op jit(solution)/shard_map/ppermute | solution.py:247
  224.4 8.3 %collective-permute-start.20 = (f32[128,128]{1,0:T(8,128)}, f32[128,128]{1,0:T(8,128)}, u32[]{:S(2)}, u32[]{:S(2)}) collective-permute-start(f32[128,128]{1,0:T(8,128)} %get-tuple-element.84), channel_id=1, source_target_pairs={{0,64},{32,96},{64,0},{96,32},{1,65},{33,97},{65,1},{97,33},{2,66}... | collective-permute-start | bytes 196616 | tf_op jit(solution)/shard_map/ppermute | solution.py:247
  227.6 5.0 %collective-permute-start.21 = (f32[128,128]{1,0:T(8,128)S(1)}, f32[128,128]{1,0:T(8,128)}, u32[]{:S(2)}, u32[]{:S(2)}) collective-permute-start(f32[128,128]{1,0:T(8,128)S(1)} %get-tuple-element.83), channel_id=1, source_target_pairs={{0,32},{32,0},{64,96},{96,64},{1,33},{33,1},{65,97},{97,65},{2,34}... | collective-permute-start | bytes 196616 | tf_op jit(solution)/shard_map/ppermute | solution.py:247
  (15 other events, 420.9 us)
where the time goes:
time: 235 us; the launch traced here: 234 us
  starting transfers between devices  135 us (57%)
  blocking collectives  22.8 us (10%)
  waiting for transfers between devices  22.5 us (10%)
  other arithmetic  19.6 us (8%)
  matrix products  17.4 us (7%)
  local copies, waits for them, and re-layouts  15.1 us (6%)
    ppermute x11, starting transfers between devices, swap(): return lax.ppermute(array, axis, SWAP)  52.1 us
    ppermute x3, starting transfers between devices, ring(): backward = lax.ppermute(backward, 'zh', behind)  30.9 us
    all_gather x1, blocking collectives, side_by_side(): result, at, done = (lax.all_gather(both, axis, axis=dim, tiled=True), 0, [])  22.8 us
    ppermute x3, starting transfers between devices, shared_out(): lax.ppermute(result[:, r * width:(r + 1) * width], ('zl', 'core'), [(i, i...  20.8 us
    all_to_all x2, starting transfers between devices, exchange(): return lax.all_to_all(array, 'exp', split_axis=0, concat_axis=0, tiled=True)  14.2 us
    ppermute x3, starting transfers between devices, ring(): forward = lax.ppermute(forward, 'zh', ahead)  9.65 us
    ppermute x3, waiting for transfers between devices, ring(): backward = lax.ppermute(backward, 'zh', behind)  9.35 us
    unnamed x39, local copies, waits for them, and re-layouts  9.26 us
  transfers between devices with their start and end apart: 24, of which 5 were waited for; matrix products, arithmetic and copies ran while one was open for 21% of the time, Pallas kernels for 0%

commit v1 on v0

--- a/solution.py
+++ b/solution.py
@@ -7,17 +7,6 @@
 
 
 HIGHEST = lax.Precision.HIGHEST
-
-
-def side_by_side(arrays, axis, dim, along):
-    columns = [a.reshape(*a.shape[:along], -1) for a in arrays]
-    both = jnp.concatenate(columns, axis=along)
-    result, at, done = (lax.all_gather(both, axis, axis=dim, tiled=True), 0, [])
-    for a, column in zip(arrays, columns):
-        section = result[..., at : at + column.shape[along]]
-        done.append(section.reshape(*section.shape[:along], *a.shape[along:]))
-        at += column.shape[along]
-    return tuple(done)
 
 
 def block_chain(running, pieces):
@@ -82,7 +71,6 @@
 
 CTX = ("zh", "zl", "core")
 SWAP = ((0, 1), (1, 0))
-CHUNKS = 1
 
 
 def swap(array, axis):
@@ -92,23 +80,6 @@
 def four(array, across):
     beside = swap(array, "core")
     return (array, beside, across, swap(across, "core"))
-
-
-def ring(array):
-    count = lax.axis_size("zh")
-    rows = array.shape[0]
-    ahead = [(i, (i + 1) % count) for i in range(count)]
-    behind = [(i, (i - 1) % count) for i in range(count)]
-    yield 0, 0, array
-    forward, backward = array, array
-    for step in range(1, count // 2):
-        forward = lax.ppermute(forward, "zh", ahead)
-        backward = lax.ppermute(backward, "zh", behind)
-        yield -step, 0, forward
-        yield step, 0, backward
-    half = rows // 2
-    yield -(count // 2), 0, lax.ppermute(forward[:half], "zh", ahead)
-    yield count // 2, half, lax.ppermute(backward[half:], "zh", behind)
 
 
 def absolute(pieces):
@@ -139,7 +110,7 @@
     return jax.tree.map(lambda a, b: jnp.where(flag, a, b), left, right)
 
 
-def carry(total_log, final):
+def group_state(total_log, final):
     own = (total_log, final)
     before = jax.tree.map(jnp.zeros_like, own)
     for axis in ("core", "zl"):
@@ -147,61 +118,78 @@
         later = lax.axis_index(axis) == 1
         before = chosen(later, joined(other, before), before)
         own = chosen(later, joined(other, own), joined(own, other))
-    logs, states = side_by_side((own[0][None], own[1][None]), "zh", 0, 2)
+    return own, before
+
+
+def upper(array):
+    return lax.reduce_precision(array, 8, 7)
+
+
+def state_rows(log, state, width):
+    flat = state.reshape(-1, width)
+    high = upper(flat)
+    first = upper(log)
+    second = upper(log - first)
+    logs = jnp.stack([first, second, log - first - second])
+    logs = jnp.pad(logs, ((0, flat.shape[0] - 3), (0, width - log.shape[0])))
+    return jnp.concatenate([high, flat - high, logs], axis=0).astype(jnp.bfloat16)
+
+
+def read_rows(rows, shape):
+    count, _, width = rows.shape
+    parts = rows.reshape(count, 3, -1, width).astype(jnp.float32)
+    logs = jnp.sum(parts[:, 2, :3, : shape[0]], axis=1)
+    return logs, (parts[:, 0] + parts[:, 1]).reshape(count, *shape)
+
+
+def state_ahead(offsets, logs, states, before):
+    place = lax.axis_index("zh")
     count = lax.axis_size("zh")
-    place = lax.axis_index("zh")
-    source = lax.broadcasted_iota(jnp.int32, (count, count), 0)
-    target = lax.broadcasted_iota(jnp.int32, (count, count), 1)
-    between = ((target > source) & (target < place)).astype(jnp.float32)
-    log_span = jnp.dot(between, logs, precision=HIGHEST, preferred_element_type=jnp.float32)
-    earlier = lax.broadcasted_iota(jnp.int32, (count, 1), 0) < place
-    factor = jnp.where(earlier, jnp.exp(log_span), 0.0)
+    source = (place + jnp.array([o + count for o in offsets], jnp.int32)) % count
+    earlier = source < place
+    between = (source[None, :] > source[:, None]) & earlier[None, :]
+    span = jnp.sum(jnp.where(between[:, :, None], logs[None], 0.0), axis=1)
+    factor = jnp.where(earlier[:, None], jnp.exp(span), 0.0)
     outside = jnp.sum(factor[:, :, None, None] * states, axis=0)
-    return joined((jnp.zeros_like(total_log), outside), before)[1]
-
-
-def route(expert_ids, route_weights, expert_count, rows):
+    return joined((jnp.zeros_like(before[0]), outside), before)[1]
+
+
+def route(expert_ids, route_weights, expert_count, capacity):
     group_size = expert_ids.shape[0]
-    quarter = CHUNKS * rows
+    quarter = capacity // 4
     part = lax.axis_index("zl") * 2 + lax.axis_index("core")
     assigned = expert_ids.reshape(group_size * 2)
     onehot = (
         assigned[:, None] == lax.broadcasted_iota(jnp.int32, (group_size * 2, expert_count), 1)
     ).astype(jnp.int32)
     earlier_count = jnp.cumsum(onehot, axis=0) - onehot
-    slot = jnp.sum(earlier_count * onehot, axis=1) - part * quarter
-    position = jnp.where((slot >= 0) & (slot < quarter), assigned * quarter + slot, -1)
-    matches = (
-        position[:, None]
-        == lax.broadcasted_iota(jnp.int32, (group_size * 2, expert_count * quarter), 1)
-    ).astype(jnp.float32)
-    shape = (group_size, 2, expert_count, CHUNKS, rows)
-    dispatch = jnp.sum(matches.reshape(shape), axis=1).astype(jnp.bfloat16)
+    slot = jnp.sum(earlier_count * onehot, axis=1)
+    ours = slot - part * quarter
+    place = jnp.where((ours >= 0) & (ours < quarter), assigned * quarter + ours, -1)
+
+    def matches(position, count):
+        return (
+            position[:, None] == lax.broadcasted_iota(jnp.int32, (group_size * 2, count), 1)
+        ).astype(jnp.float32)
+
+    dispatch = jnp.sum(
+        matches(place, expert_count * quarter).reshape(group_size, 2, -1), axis=1
+    ).astype(jnp.bfloat16)
     combine = jnp.sum(
-        (matches * route_weights.reshape(group_size * 2)[:, None]).reshape(shape), axis=1
-    )
-    return dispatch, combine
-
-
-def exchange(array):
-    return lax.all_to_all(array, "exp", split_axis=0, concat_axis=0, tiled=True)
-
-
-def send_slots(moe_tokens, dispatch):
-    group_size, expert_count, _, rows = dispatch.shape
-    packed = []
-    for chunk in range(CHUNKS):
-        onehot = jnp.broadcast_to(
-            dispatch[:, :, chunk, :][:, :, None, :], (group_size, expert_count, 2, rows)
-        )
-        packed.append(
-            jnp.einsum(
-                "iehs,id->ehsd", onehot, moe_tokens, preferred_element_type=jnp.float32
-            )
-            .astype(jnp.bfloat16)
-            .reshape(2 * expert_count, rows, -1)
-        )
-    return packed
+        (
+            matches(assigned * capacity + slot, expert_count * capacity)
+            * route_weights.reshape(group_size * 2)[:, None]
+        ).reshape(group_size, 2, -1),
+        axis=1,
+    )
+    return dispatch.reshape(group_size, expert_count, quarter), combine
+
+
+def packed_slots(moe_tokens, dispatch):
+    group_size, expert_count, rows = dispatch.shape
+    onehot = jnp.broadcast_to(dispatch[:, :, None, :], (group_size, expert_count, 2, rows))
+    packed = jnp.einsum("iehs,id->ehsd", onehot, moe_tokens, preferred_element_type=jnp.float32)
+    return packed.astype(jnp.bfloat16).reshape(2 * expert_count, rows, -1)
 
 
 def hidden_units(arrived, weights, hidden_count):
@@ -215,39 +203,47 @@
     return absolute(pieces).reshape(4 * hidden_count, -1)
 
 
-def down_sums(hidden, down):
+def down_sums(hidden, extra, down):
     place = lax.axis_index("zh")
     count = lax.axis_size("zh")
     size = hidden.shape[0]
-    total = 0.0
-    for offset, first, shard in ring(hidden):
+    head = extra.shape[0]
+    ahead = [(i, (i + 1) % count) for i in range(count)]
+    behind = [(i, (i - 1) % count) for i in range(count)]
+
+    def product(offset, first, shard):
         start = (place + (offset + count)) % count * size + first
         rows = lax.dynamic_slice_in_dim(down, start, shard.shape[0], 0)
-        total = total + lax.dot_general(
+        return lax.dot_general(
             shard, rows, (((0,), (0,)), ((), ())), preferred_element_type=jnp.float32
         )
-    return total
-
-
-def combined(returned, combine):
-    group_size, expert_count, rows = combine.shape
-    summed = jnp.sum(returned.reshape(expert_count, 2, rows, -1), axis=1)
-    return jnp.dot(
-        combine.reshape(group_size, expert_count * rows),
-        summed.reshape(expert_count * rows, -1),
-        precision=HIGHEST,
-        preferred_element_type=jnp.float32,
-    )
-
-
-def shared_out(result):
-    width = result.shape[1] // 4
-    total = result[:, :width]
-    for r in (3, 2, 1):
-        total = total + lax.ppermute(
-            result[:, r * width : (r + 1) * width], ("zl", "core"), [(i, i ^ r) for i in range(4)]
-        )
-    return total.astype(jnp.bfloat16)
+
+    def both(step, near):
+        return product(-step, 0, near[0][head:]) + product(step, 0, near[1][head:])
+
+    forward = backward = jnp.concatenate([extra, hidden], axis=0)
+    offsets, extras = [], []
+    total = product(0, 0, hidden)
+    last = count // 2
+    for step in range(1, last):
+        forward = lax.ppermute(forward, "zh", ahead)
+        backward = lax.ppermute(backward, "zh", behind)
+        offsets += [-step, step]
+        extras += [forward, backward]
+        total = total + both(step, (forward, backward))
+    half = (size + head) // 32 * 16
+    forward = lax.ppermute(forward[:half], "zh", ahead)
+    backward = lax.ppermute(backward[half:], "zh", behind)
+    offsets.append(-last)
+    extras.append(forward)
+    total = total + product(-last, 0, forward[head:]) + product(last, half - head, backward)
+    return total, offsets, extras
+
+
+def ordered(blocks):
+    for axis, dim in (("zl", 0), ("core", 1)):
+        blocks = jnp.where(lax.axis_index(axis) == 0, blocks, jnp.flip(blocks, dim))
+    return blocks
 
 
 def layer(
@@ -264,18 +260,20 @@
     up_proj,
     down_proj,
 ):
+    group_size = moe_tokens.shape[0]
     expert_count = lax.axis_size("exp") // 2
-    rows = min(moe_tokens.shape[0], 4 * moe_tokens.shape[0] // expert_count) // 4 // CHUNKS
+    capacity = min(group_size, 4 * group_size // expert_count)
+    rows = capacity // 4
     hidden_count = gate_proj.shape[2]
     gate, up, down = gate_proj[0], up_proj[0], down_proj[0]
     gate_across = swap(gate, "zl")
-    up_across = swap(up, "zl")
-    dispatch, combine = route(expert_ids, route_weights, expert_count, rows)
-    packed = send_slots(moe_tokens, dispatch)
+    dispatch, combine = route(expert_ids, route_weights, expert_count, capacity)
+    packed = packed_slots(moe_tokens, dispatch)
     packed, gate, up, down, seq_inputs, step_size = lax.optimization_barrier(
         (packed, gate, up, down, seq_inputs, step_size)
     )
-    arrived = [exchange(chunk) for chunk in packed]
+    arrived = lax.all_to_all(packed, "exp", split_axis=0, concat_axis=0, tiled=True)
+    up_across = swap(up, "zl")
     down_across = swap(down, "zl")
     gates = four(gate, gate_across)
     ups = four(up, up_across)
@@ -286,21 +284,31 @@
     local_mix, cumulative, block_ends, entering, final = mixer_prepare(
         seq_inputs, step_size, write_map, read_map, decay_log
     )
-    sums = [
-        down_sums(
-            hidden_units(a.reshape(2 * expert_count * rows, -1), weights, hidden_count),
-            down_columns,
-        )
-        for a in arrived
-    ]
-    total_log = jnp.sum(block_ends, axis=1)
-    returned = [exchange(part.reshape(2 * expert_count, rows, -1)) for part in sums]
-    state_before = carry(total_log, final)
+    group, before = group_state(jnp.sum(block_ends, axis=1), final)
+    hidden = hidden_units(arrived.reshape(2 * expert_count * rows, -1), weights, hidden_count)
+    state_part = state_rows(*group, hidden.shape[1])
+    sums, offsets, extras = down_sums(hidden, state_part, down_columns)
+    width = down.shape[1]
+    blocks = sums.reshape(2 * expert_count, rows, 4, width).transpose(2, 0, 1, 3)
+    blocks = ordered(blocks.reshape(2, 2, 2 * expert_count, rows, width))
+    blocks = blocks.transpose(2, 0, 1, 3, 4).reshape(8 * expert_count, rows, width)
+    blocks, *extras = lax.optimization_barrier((blocks, *extras))
+    returned = lax.all_to_all(
+        blocks, ("exp", "zl", "core"), split_axis=0, concat_axis=0, tiled=True
+    )
+    head = state_part.shape[0]
+    states = jnp.stack([message[:head] for message in extras])
+    state_before = state_ahead(offsets, *read_rows(states, final.shape), before)
     mixer_output = mixer_finish(
         local_mix, cumulative, block_ends, entering, state_before, read_map, seq_inputs, skip_gain
     )
-    result = sum(combined(part, combine[:, :, chunk]) for chunk, part in enumerate(returned))
-    expert_output = shared_out(result)
+    summed = jnp.sum(returned.reshape(expert_count, 2, capacity, width), axis=1)
+    expert_output = jnp.dot(
+        combine,
+        summed.reshape(expert_count * capacity, width),
+        precision=HIGHEST,
+        preferred_element_type=jnp.float32,
+    ).astype(jnp.bfloat16)
     return (mixer_output, expert_output)
 
 

time: 235 us -> 210 us (0.89)
  waiting for transfers between devices: 22.5 us -> 69.5 us
  starting transfers between devices: 135 us -> 91.2 us
  blocking collectives: 22.8 us -> 0 us
  matrix products: 17.4 us -> 13.1 us
    ppermute x11 -> x8, starting transfers between devices: 68.9 us -> 25.4 us  [the longest x3 12.3 us: down_sums(): backward = lax.ppermute(backward, 'zh', behind)]
    ppermute x11, waiting for transfers between devices: 3.26 us -> 26.5 us  [swap(): return lax.ppermute(array, axis, SWAP)]
    all_gather x1 -> x0, blocking collectives: 22.8 us -> none  [side_by_side(): result, at, done = (lax.all_gather(both, axis, axis=dim, tiled=True), 0, [])]
    all_to_all x2, waiting for transfers between devices: 0.01 us -> 15.3 us  [the longest x1 15.3 us: layer(): lax.all_to_all(blocks, ('exp', 'zl', 'core'), split_axis=0, concat_axis=0...]
    ppermute x11, starting transfers between devices: 52.1 us -> 40.5 us  [swap(): return lax.ppermute(array, axis, SWAP)]
    all_to_all x2, starting transfers between devices: 14.2 us -> 25.2 us  [the longest x1 21.2 us: layer(): lax.all_to_all(blocks, ('exp', 'zl', 'core'), split_axis=0, concat_axis=0...]
    ppermute x11 -> x8, waiting for transfers between devices: 19.2 us -> 27.7 us  [the longest x3 14.6 us: down_sums(): forward = lax.ppermute(forward, 'zh', ahead)]
    dot_general x2, matrix products: 7 us -> 4.61 us  [hidden_units(): lax.dot_general(weight, arrived, (((0,), (1,)), ((), ())), preferred_elem...]
  transfers between devices with their start and end apart: 24 -> 21, of which waited for: 5 -> 9; matrix products, arithmetic and copies ran while one was open for 21% -> 18% of each run, Pallas kernels for 0% -> 0%
where the time goes in v1:
time: 210 us; the launch traced here: 209 us
  starting transfers between devices  91.2 us (43%)
  waiting for transfers between devices  69.5 us (33%)
  other arithmetic  17.7 us (8%)
  local copies, waits for them, and re-layouts  15.8 us (8%)
  matrix products  13.1 us (6%)
    ppermute x11, starting transfers between devices, swap(): return lax.ppermute(array, axis, SWAP)  40.5 us
    ppermute x11, waiting for transfers between devices, swap(): return lax.ppermute(array, axis, SWAP)  26.5 us
    all_to_all x1, starting transfers between devices, layer(): lax.all_to_all(blocks, ('exp', 'zl', 'core'), split_axis=0, concat_axis=0...  21.2 us
    all_to_all x1, waiting for transfers between devices, layer(): lax.all_to_all(blocks, ('exp', 'zl', 'core'), split_axis=0, concat_axis=0...  15.3 us
    ppermute x3, waiting for transfers between devices, down_sums(): forward = lax.ppermute(forward, 'zh', ahead)  14.6 us
    ppermute x3, starting transfers between devices, down_sums(): backward = lax.ppermute(backward, 'zh', behind)  12.3 us
    ppermute x3, waiting for transfers between devices, down_sums(): backward = lax.ppermute(backward, 'zh', behind)  11.8 us
    unnamed x70, local copies, waits for them, and re-layouts  9.21 us
  transfers between devices with their start and end apart: 21, of which 9 were waited for; matrix products, arithmetic and copies ran while one was open for 18% of the time, Pallas kernels for 0%

profile of v1, /device:TPU:1, one launch (start us, length us, event | category | flops | bytes accessed | tf_op | source)
XLA Modules:
  0.0 209.1 jit_solution(1771413123306504763)
XLA Ops:
  6.3 16.0 %collective-permute-start.3 = (bf16[4096,112]{0,1:T(8,128)(2,1)}, bf16[4096,112]{0,1:T(8,128)(2,1)}, u32[]{:S(2)}, u32[]{:S(2)}) collective-permute-start(bf16[4096,112]{0,1:T(8,128)(2,1)} %bitcast.6), channel_id=1, source_target_pairs={{0,32},{32,0},{1,33},{33,1},{2,34},{34,2},{3,35},{35,3},{4,36},{36... | collective-permute-start | bytes 2752520 | tf_op jit(solution)/shard_map/ppermute | solution.py:77
  24.2 3.4 %collective-permute-start.4 = (bf16[4096,112]{0,1:T(8,128)(2,1)}, bf16[4096,112]{0,1:T(8,128)(2,1)}, u32[]{:S(2)}, u32[]{:S(2)}) collective-permute-start(bf16[4096,112]{0,1:T(8,128)(2,1)} %bitcast.5), channel_id=1, source_target_pairs={{0,64},{64,0},{1,65},{65,1},{2,66},{66,2},{3,67},{67,3},{4,68},{68... | collective-permute-start | bytes 2752520 | tf_op jit(solution)/shard_map/ppermute | solution.py:77
  27.7 2.4 %reduce-window.16 = f32[4,2,2,128]{3,2,1,0:T(2,128)S(1)} reduce-window(f32[4,2,2,128]{3,2,1,0:T(2,128)S(1)} %reshape.401, f32[]{:T(128)} %constant.121.clone.1), window={size=1x1x1x128 pad=0_0x0_0x0_0x127_0}, to_apply=%region_4.5 | reduce-window | flops 260096 | bytes 16388 | tf_op jit(solution)/shard_map/reduce-window.2
  32.9 2.5 %collective-permute-start = (f32[4,1025]{1,0:T(4,128)S(1)}, f32[4,1025]{1,0:T(4,128)S(1)}, u32[]{:S(2)}, u32[]{:S(2)}) collective-permute-start(f32[4,1025]{1,0:T(4,128)S(1)} %pad_maximum_fusion.6), channel_id=1, source_target_pairs={{0,32},{32,0},{1,33},{33,1},{2,34},{34,2},{3,35},{35,3},{4,36},{36... | collective-permute-start | bytes 49208 | tf_op jit(solution)/shard_map/ppermute | solution.py:77
  35.4 4.0 %all-to-all-start = ((bf16[32,8,4096]{2,1,0:T(8,128)(2,1)}), bf16[32,8,4096]{2,1,0:T(8,128)(2,1)S(1)}, u32[]{:S(2)}, u32[]{:S(2)}) async-start(bf16[32,8,4096]{2,1,0:T(8,128)(2,1)} %bitcast.4), calls=%async_computation | async-start | bytes 4194304 | tf_op jit(solution)/shard_map/all_to_all | solution.py:275
  50.7 15.8 %collective-permute-done.1 = f32[4,1025]{1,0:T(4,128)} collective-permute-done((f32[4,1025]{1,0:T(4,128)}, f32[4,1025]{1,0:T(4,128)}, u32[]{:S(2)}, u32[]{:S(2)}) %collective-permute-start.1) | collective-permute-done | bytes 16432 | tf_op jit(solution)/shard_map/ppermute | solution.py:77
  71.8 2.8 %collective-permute-start.2 = (bf16[4096,112]{0,1:T(8,128)(2,1)}, bf16[4096,112]{0,1:T(8,128)(2,1)S(1)}, u32[]{:S(2)}, u32[]{:S(2)}) collective-permute-start(bf16[4096,112]{0,1:T(8,128)(2,1)} %bitcast.5), channel_id=1, source_target_pairs={{0,32},{32,0},{1,33},{33,1},{2,34},{34,2},{3,35},{35,3},{4,36},{36... | collective-permute-start | bytes 2752520 | tf_op jit(solution)/shard_map/ppermute | solution.py:77
  76.5 2.4 %collective-permute-start.6 = (bf16[4096,112]{0,1:T(8,128)(2,1)}, bf16[4096,112]{0,1:T(8,128)(2,1)S(1)}, u32[]{:S(2)}, u32[]{:S(2)}) collective-permute-start(bf16[4096,112]{0,1:T(8,128)(2,1)} %collective-permute-done.4), channel_id=1, source_target_pairs={{0,32},{32,0},{1,33},{33,1},{2,34},{34,2},{3,35},{35,3},{4,36},{36... | collective-permute-start | bytes 2752520 | tf_op jit(solution)/shard_map/ppermute | solution.py:77
  79.0 10.7 %collective-permute-done.9 = bf16[3584,128]{1,0:T(8,128)(2,1)} collective-permute-done((bf16[3584,128]{1,0:T(8,128)(2,1)}, bf16[3584,128]{1,0:T(8,128)(2,1)}, u32[]{:S(2)}, u32[]{:S(2)}) %collective-permute-start.9) | collective-permute-done | bytes 917536 | tf_op jit(solution)/shard_map/ppermute | solution.py:77
  89.7 3.6 %collective-permute-start.10 = (bf16[3584,128]{1,0:T(8,128)(2,1)}, bf16[3584,128]{1,0:T(8,128)(2,1)}, u32[]{:S(2)}, u32[]{:S(2)}) collective-permute-start(bf16[3584,128]{1,0:T(8,128)(2,1)} %collective-permute-done.9), channel_id=1, source_target_pairs={{0,32},{32,0},{1,33},{33,1},{2,34},{34,2},{3,35},{35,3},{4,36},{36... | collective-permute-start | bytes 2752520 | tf_op jit(solution)/shard_map/ppermute | solution.py:77
  95.6 2.2 %constant_dynamic-update-slice_fusion.1 = bf16[3584,512]{1,0:T(8,128)(2,1)} fusion(bf16[3584,512]{1,0:T(8,128)(2,1)} %constant_dynamic-update-slice_fusion.2, bf16[3584,128]{1,0:T(8,128)(2,1)} %collective-permute-done.9), kind=kLoop, calls=%fused_computation.99 | loop fusion | bytes 1835008
  97.8 3.4 %pad_maximum_fusion = bf16[4096,448]{0,1:T(8,128)(2,1)} fusion(bf16[4096,112]{0,1:T(8,128)(2,1)} %collective-permute-done.3, bf16[4096,112]{0,1:T(8,128)(2,1)S(1)} %collective-permute-done.2, bf16[4096,112]{0,1:T(8,128)(2,1)} %bitcast.6, bf16[4096,112]{0,1:T(8,128)(2,1)} %bitcast.5), kind=kLoop, calls=%fused_computation.5 | loop fusion | flops 14680064 | bytes 7340032 | tf_op jit(solution)/shard_map/concatenate | solution.py:281
  101.2 3.2 %pad_maximum_fusion.1 = bf16[4096,448]{0,1:T(8,128)(2,1)} fusion(bf16[4096,112]{0,1:T(8,128)(2,1)S(1)} %collective-permute-done.7, bf16[4096,112]{0,1:T(8,128)(2,1)S(1)} %collective-permute-done.6, bf16[4096,112]{0,1:T(8,128)(2,1)} %collective-permute-done.5, bf16[4096,112]{0,1:T(8,128)(2,1)} %collective-permute-done.4), kind=kLoop, calls=%fused_computation.6 | loop fusion | flops 14680064 | bytes 7340032 | tf_op jit(solution)/shard_map/concatenate | solution.py:281
  104.4 3.3 %fusion.3 = f32[2,2,112,256]{3,2,1,0:T(8,128)S(1)} fusion(bf16[2,2,112,4096]{3,2,1,0:T(8,128)(2,1)} %bitcast.160, bf16[32,8,4096]{2,1,0:T(8,128)(2,1)S(1)} %all-to-all-done), kind=kOutput, calls=%fused_computation.9 | convolution fusion | flops 939524096 | bytes 6225920 | tf_op jit(solution)/shard_map/dot_general | solution.py:198
  109.3 5.3 %collective-permute-start.12 = (bf16[496,256]{1,0:T(8,128)(2,1)S(1)}, bf16[496,256]{1,0:T(8,128)(2,1)S(1)}, u32[]{:S(2)}, u32[]{:S(2)}) collective-permute-start(bf16[496,256]{1,0:T(8,128)(2,1)S(1)} %pad_maximum_fusion.2), channel_id=1, source_target_pairs={{0,896},{128,0},{256,128},{384,256},{512,384},{640,512},{768,640},... | collective-permute-start | bytes 761864 | tf_op jit(solution)/shard_map/ppermute | solution.py:230
  118.0 7.7 %collective-permute-done.12 = bf16[496,256]{1,0:T(8,128)(2,1)S(1)} collective-permute-done((bf16[496,256]{1,0:T(8,128)(2,1)S(1)}, bf16[496,256]{1,0:T(8,128)(2,1)S(1)}, u32[]{:S(2)}, u32[]{:S(2)}) %collective-permute-start.12) | collective-permute-done | bytes 253984 | tf_op jit(solution)/shard_map/ppermute | solution.py:230
  125.7 4.1 %collective-permute-start.14 = (bf16[496,256]{1,0:T(8,128)(2,1)S(1)}, bf16[496,256]{1,0:T(8,128)(2,1)S(1)}, u32[]{:S(2)}, u32[]{:S(2)}) collective-permute-start(bf16[496,256]{1,0:T(8,128)(2,1)S(1)} %collective-permute-done.12), channel_id=1, source_target_pairs={{0,896},{128,0},{256,128},{384,256},{512,384},{640,512},{768,640},... | collective-permute-start | bytes 761864 | tf_op jit(solution)/shard_map/ppermute | solution.py:230
  134.0 4.1 %collective-permute-done.14 = bf16[496,256]{1,0:T(8,128)(2,1)S(1)} collective-permute-done((bf16[496,256]{1,0:T(8,128)(2,1)S(1)}, bf16[496,256]{1,0:T(8,128)(2,1)S(1)}, u32[]{:S(2)}, u32[]{:S(2)}) %collective-permute-start.14) | collective-permute-done | bytes 253984 | tf_op jit(solution)/shard_map/ppermute | solution.py:230
  138.1 2.9 %collective-permute-start.16 = (bf16[496,256]{1,0:T(8,128)(2,1)S(1)}, bf16[496,256]{1,0:T(8,128)(2,1)S(1)}, u32[]{:S(2)}, u32[]{:S(2)}) collective-permute-start(bf16[496,256]{1,0:T(8,128)(2,1)S(1)} %collective-permute-done.14), channel_id=1, source_target_pairs={{0,896},{128,0},{256,128},{384,256},{512,384},{640,512},{768,640},... | collective-permute-start | bytes 761864 | tf_op jit(solution)/shard_map/ppermute | solution.py:230
  141.3 5.9 %collective-permute-done.13 = bf16[496,256]{1,0:T(8,128)(2,1)S(1)} collective-permute-done((bf16[496,256]{1,0:T(8,128)(2,1)S(1)}, bf16[496,256]{1,0:T(8,128)(2,1)S(1)}, u32[]{:S(2)}, u32[]{:S(2)}) %collective-permute-start.13) | collective-permute-done | bytes 253984 | tf_op jit(solution)/shard_map/ppermute | solution.py:229
  149.9 6.9 %collective-permute-done.15 = bf16[496,256]{1,0:T(8,128)(2,1)S(1)} collective-permute-done((bf16[496,256]{1,0:T(8,128)(2,1)S(1)}, bf16[496,256]{1,0:T(8,128)(2,1)S(1)}, u32[]{:S(2)}, u32[]{:S(2)}) %collective-permute-start.15) | collective-permute-done | bytes 253984 | tf_op jit(solution)/shard_map/ppermute | solution.py:229
  158.8 5.5 %collective-permute-start.18 = (bf16[256,256]{1,0:T(8,128)(2,1)S(1)}, bf16[256,256]{1,0:T(8,128)(2,1)S(1)}, u32[]{:S(2)}, u32[]{:S(2)}) collective-permute-start(bf16[256,256]{1,0:T(8,128)(2,1)S(1)} %slice.168), channel_id=1, source_target_pairs={{0,896},{128,0},{256,128},{384,256},{512,384},{640,512},{768,640},... | collective-permute-start | bytes 393224 | tf_op jit(solution)/shard_map/ppermute | solution.py:236
  167.9 21.2 %all-to-all-start.1 = ((f32[128,8,128]{2,1,0:T(8,128)}), f32[128,8,128]{2,1,0:T(8,128)S(1)}, u32[]{:S(2)}, u32[]{:S(2)}) async-start(f32[128,8,128]{2,1,0:T(8,128)} %bitcast.37), calls=%async_computation.1 | async-start | bytes 1048576 | tf_op jit(solution)/shard_map/all_to_all | solution.py:296
  192.7 15.3 %all-to-all-done.1 = f32[128,8,128]{2,1,0:T(8,128)S(1)} async-done(((f32[128,8,128]{2,1,0:T(8,128)}), f32[128,8,128]{2,1,0:T(8,128)S(1)}, u32[]{:S(2)}, u32[]{:S(2)}) %all-to-all-start.1) | async-done | bytes 524320 | tf_op jit(solution)/shard_map/all_to_all | solution.py:296
  (213 shorter events, 52.9 us)
Async XLA Ops:
  0.6 30.5 %copy-start.5 = (bf16[512,256]{1,0:T(8,128)(2,1)S(1)}, bf16[512,256]{1,0:T(8,128)(2,1)}, u32[]{:S(2)}) copy-start(bf16[512,256]{1,0:T(8,128)(2,1)} %param.15) | copy-start | bytes 786436
  0.7 31.0 %copy-start.8 = (bf16[16,512]{1,0:T(8,128)(2,1)S(1)}, bf16[16,512]{1,0:T(8,128)(2,1)}, u32[]{:S(2)}) copy-start(bf16[16,512]{1,0:T(8,128)(2,1)} %param.17) | copy-start | bytes 49156
  6.3 91.5 %collective-permute-start.3 = (bf16[4096,112]{0,1:T(8,128)(2,1)}, bf16[4096,112]{0,1:T(8,128)(2,1)}, u32[]{:S(2)}, u32[]{:S(2)}) collective-permute-start(bf16[4096,112]{0,1:T(8,128)(2,1)} %bitcast.6), channel_id=1, source_target_pairs={{0,32},{32,0},{1,33},{33,1},{2,34},{34,2},{3,35},{35,3},{4,36},{36... | collective-permute-start | bytes 2752520 | tf_op jit(solution)/shard_map/ppermute | solution.py:77
  22.3 49.5 %collective-permute-start.5 = (bf16[4096,112]{0,1:T(8,128)(2,1)}, bf16[4096,112]{0,1:T(8,128)(2,1)}, u32[]{:S(2)}, u32[]{:S(2)}) collective-permute-start(bf16[4096,112]{0,1:T(8,128)(2,1)} %bitcast.6), channel_id=1, source_target_pairs={{0,64},{64,0},{1,65},{65,1},{2,66},{66,2},{3,67},{67,3},{4,68},{68... | collective-permute-start | bytes 2752520 | tf_op jit(solution)/shard_map/ppermute | solution.py:77
  24.2 50.4 %collective-permute-start.4 = (bf16[4096,112]{0,1:T(8,128)(2,1)}, bf16[4096,112]{0,1:T(8,128)(2,1)}, u32[]{:S(2)}, u32[]{:S(2)}) collective-permute-start(bf16[4096,112]{0,1:T(8,128)(2,1)} %bitcast.5), channel_id=1, source_target_pairs={{0,64},{64,0},{1,65},{65,1},{2,66},{66,2},{3,67},{67,3},{4,68},{68... | collective-permute-start | bytes 2752520 | tf_op jit(solution)/shard_map/ppermute | solution.py:77
  30.8 39.5 %copy-start.15 = (f32[4]{0:T(128)}, f32[4]{0:T(128)S(1)}, u32[]{:S(2)}) copy-start(f32[4]{0:T(128)S(1)} %get-tuple-element.116) | copy-start | bytes 52
  32.9 13.9 %collective-permute-start = (f32[4,1025]{1,0:T(4,128)S(1)}, f32[4,1025]{1,0:T(4,128)S(1)}, u32[]{:S(2)}, u32[]{:S(2)}) collective-permute-start(f32[4,1025]{1,0:T(4,128)S(1)} %pad_maximum_fusion.6), channel_id=1, source_target_pairs={{0,32},{32,0},{1,33},{33,1},{2,34},{34,2},{3,35},{35,3},{4,36},{36... | collective-permute-start | bytes 49208 | tf_op jit(solution)/shard_map/ppermute | solution.py:77
  35.4 69.0 %all-to-all-start = ((bf16[32,8,4096]{2,1,0:T(8,128)(2,1)}), bf16[32,8,4096]{2,1,0:T(8,128)(2,1)S(1)}, u32[]{:S(2)}, u32[]{:S(2)}) async-start(bf16[32,8,4096]{2,1,0:T(8,128)(2,1)} %bitcast.4), calls=%async_computation | async-start | bytes 4194304 | tf_op jit(solution)/shard_map/all_to_all | solution.py:275
  39.5 37.1 %collective-permute-start.8 = (bf16[3584,128]{1,0:T(8,128)(2,1)}, bf16[3584,128]{1,0:T(8,128)(2,1)}, u32[]{:S(2)}, u32[]{:S(2)}) collective-permute-start(bf16[3584,128]{1,0:T(8,128)(2,1)} %bitcast.167), channel_id=1, source_target_pairs={{0,32},{32,0},{1,33},{33,1},{2,34},{34,2},{3,35},{35,3},{4,36},{36... | collective-permute-start | bytes 2752520 | tf_op jit(solution)/shard_map/ppermute | solution.py:77
  48.1 18.4 %collective-permute-start.1 = (f32[4,1025]{1,0:T(4,128)}, f32[4,1025]{1,0:T(4,128)}, u32[]{:S(2)}, u32[]{:S(2)}) collective-permute-start(f32[4,1025]{1,0:T(4,128)} %pad_maximum_fusion.7), channel_id=1, source_target_pairs={{0,64},{64,0},{1,65},{65,1},{2,66},{66,2},{3,67},{67,3},{4,68},{68... | collective-permute-start | bytes 49208 | tf_op jit(solution)/shard_map/ppermute | solution.py:77
  66.5 23.2 %collective-permute-start.9 = (bf16[3584,128]{1,0:T(8,128)(2,1)}, bf16[3584,128]{1,0:T(8,128)(2,1)}, u32[]{:S(2)}, u32[]{:S(2)}) collective-permute-start(bf16[3584,128]{1,0:T(8,128)(2,1)} %bitcast.169), channel_id=1, source_target_pairs={{0,64},{64,0},{1,65},{65,1},{2,66},{66,2},{3,67},{67,3},{4,68},{68... | collective-permute-start | bytes 2752520 | tf_op jit(solution)/shard_map/ppermute | solution.py:77
  71.8 26.0 %collective-permute-start.2 = (bf16[4096,112]{0,1:T(8,128)(2,1)}, bf16[4096,112]{0,1:T(8,128)(2,1)S(1)}, u32[]{:S(2)}, u32[]{:S(2)}) collective-permute-start(bf16[4096,112]{0,1:T(8,128)(2,1)} %bitcast.5), channel_id=1, source_target_pairs={{0,32},{32,0},{1,33},{33,1},{2,34},{34,2},{3,35},{35,3},{4,36},{36... | collective-permute-start | bytes 2752520 | tf_op jit(solution)/shard_map/ppermute | solution.py:77
  74.6 26.6 %collective-permute-start.7 = (bf16[4096,112]{0,1:T(8,128)(2,1)}, bf16[4096,112]{0,1:T(8,128)(2,1)S(1)}, u32[]{:S(2)}, u32[]{:S(2)}) collective-permute-start(bf16[4096,112]{0,1:T(8,128)(2,1)} %collective-permute-done.5), channel_id=1, source_target_pairs={{0,32},{32,0},{1,33},{33,1},{2,34},{34,2},{3,35},{35,3},{4,36},{36... | collective-permute-start | bytes 2752520 | tf_op jit(solution)/shard_map/ppermute | solution.py:77
  76.5 24.6 %collective-permute-start.6 = (bf16[4096,112]{0,1:T(8,128)(2,1)}, bf16[4096,112]{0,1:T(8,128)(2,1)S(1)}, u32[]{:S(2)}, u32[]{:S(2)}) collective-permute-start(bf16[4096,112]{0,1:T(8,128)(2,1)} %collective-permute-done.4), channel_id=1, source_target_pairs={{0,32},{32,0},{1,33},{33,1},{2,34},{34,2},{3,35},{35,3},{4,36},{36... | collective-permute-start | bytes 2752520 | tf_op jit(solution)/shard_map/ppermute | solution.py:77
  89.7 26.9 %collective-permute-start.10 = (bf16[3584,128]{1,0:T(8,128)(2,1)}, bf16[3584,128]{1,0:T(8,128)(2,1)}, u32[]{:S(2)}, u32[]{:S(2)}) collective-permute-start(bf16[3584,128]{1,0:T(8,128)(2,1)} %collective-permute-done.9), channel_id=1, source_target_pairs={{0,32},{32,0},{1,33},{33,1},{2,34},{34,2},{3,35},{35,3},{4,36},{36... | collective-permute-start | bytes 2752520 | tf_op jit(solution)/shard_map/ppermute | solution.py:77
  109.3 16.4 %collective-permute-start.12 = (bf16[496,256]{1,0:T(8,128)(2,1)S(1)}, bf16[496,256]{1,0:T(8,128)(2,1)S(1)}, u32[]{:S(2)}, u32[]{:S(2)}) collective-permute-start(bf16[496,256]{1,0:T(8,128)(2,1)S(1)} %pad_maximum_fusion.2), channel_id=1, source_target_pairs={{0,896},{128,0},{256,128},{384,256},{512,384},{640,512},{768,640},... | collective-permute-start | bytes 761864 | tf_op jit(solution)/shard_map/ppermute | solution.py:230
  114.6 16.8 %collective-permute-start.11 = (bf16[496,256]{1,0:T(8,128)(2,1)S(1)}, bf16[496,256]{1,0:T(8,128)(2,1)S(1)}, u32[]{:S(2)}, u32[]{:S(2)}) collective-permute-start(bf16[496,256]{1,0:T(8,128)(2,1)S(1)} %pad_maximum_fusion.2), channel_id=1, source_target_pairs={{0,128},{128,256},{256,384},{384,512},{512,640},{640,768},{768,896... | collective-permute-start | bytes 761864 | tf_op jit(solution)/shard_map/ppermute | solution.py:229
  125.7 12.4 %collective-permute-start.14 = (bf16[496,256]{1,0:T(8,128)(2,1)S(1)}, bf16[496,256]{1,0:T(8,128)(2,1)S(1)}, u32[]{:S(2)}, u32[]{:S(2)}) collective-permute-start(bf16[496,256]{1,0:T(8,128)(2,1)S(1)} %collective-permute-done.12), channel_id=1, source_target_pairs={{0,896},{128,0},{256,128},{384,256},{512,384},{640,512},{768,640},... | collective-permute-start | bytes 761864 | tf_op jit(solution)/shard_map/ppermute | solution.py:230
  131.4 15.9 %collective-permute-start.13 = (bf16[496,256]{1,0:T(8,128)(2,1)S(1)}, bf16[496,256]{1,0:T(8,128)(2,1)S(1)}, u32[]{:S(2)}, u32[]{:S(2)}) collective-permute-start(bf16[496,256]{1,0:T(8,128)(2,1)S(1)} %collective-permute-done.11), channel_id=1, source_target_pairs={{0,128},{128,256},{256,384},{384,512},{512,640},{640,768},{768,896... | collective-permute-start | bytes 761864 | tf_op jit(solution)/shard_map/ppermute | solution.py:229
  138.1 20.7 %collective-permute-start.16 = (bf16[496,256]{1,0:T(8,128)(2,1)S(1)}, bf16[496,256]{1,0:T(8,128)(2,1)S(1)}, u32[]{:S(2)}, u32[]{:S(2)}) collective-permute-start(bf16[496,256]{1,0:T(8,128)(2,1)S(1)} %collective-permute-done.14), channel_id=1, source_target_pairs={{0,896},{128,0},{256,128},{384,256},{512,384},{640,512},{768,640},... | collective-permute-start | bytes 761864 | tf_op jit(solution)/shard_map/ppermute | solution.py:230
  147.3 9.5 %collective-permute-start.15 = (bf16[496,256]{1,0:T(8,128)(2,1)S(1)}, bf16[496,256]{1,0:T(8,128)(2,1)S(1)}, u32[]{:S(2)}, u32[]{:S(2)}) collective-permute-start(bf16[496,256]{1,0:T(8,128)(2,1)S(1)} %collective-permute-done.13), channel_id=1, source_target_pairs={{0,128},{128,256},{256,384},{384,512},{512,640},{640,768},{768,896... | collective-permute-start | bytes 761864 | tf_op jit(solution)/shard_map/ppermute | solution.py:229
  156.8 9.2 %collective-permute-start.17 = (bf16[240,256]{1,0:T(8,128)(2,1)S(1)}, bf16[240,256]{1,0:T(8,128)(2,1)S(1)}, u32[]{:S(2)}, u32[]{:S(2)}) collective-permute-start(bf16[240,256]{1,0:T(8,128)(2,1)S(1)} %slice.166), channel_id=1, source_target_pairs={{0,128},{128,256},{256,384},{384,512},{512,640},{640,768},{768,896... | collective-permute-start | bytes 368648 | tf_op jit(solution)/shard_map/ppermute | solution.py:235
  158.8 7.4 %collective-permute-start.18 = (bf16[256,256]{1,0:T(8,128)(2,1)S(1)}, bf16[256,256]{1,0:T(8,128)(2,1)S(1)}, u32[]{:S(2)}, u32[]{:S(2)}) collective-permute-start(bf16[256,256]{1,0:T(8,128)(2,1)S(1)} %slice.168), channel_id=1, source_target_pairs={{0,896},{128,0},{256,128},{384,256},{512,384},{640,512},{768,640},... | collective-permute-start | bytes 393224 | tf_op jit(solution)/shard_map/ppermute | solution.py:236
  167.9 40.1 %all-to-all-start.1 = ((f32[128,8,128]{2,1,0:T(8,128)}), f32[128,8,128]{2,1,0:T(8,128)S(1)}, u32[]{:S(2)}, u32[]{:S(2)}) async-start(f32[128,8,128]{2,1,0:T(8,128)} %bitcast.37), calls=%async_computation.1 | async-start | bytes 1048576 | tf_op jit(solution)/shard_map/all_to_all | solution.py:296
  (25 other events, 436.1 us)

commit v2 on v1

--- a/solution.py
+++ b/solution.py
@@ -1,6 +1,8 @@
 import jax
 import jax.numpy as jnp
 from jax import lax
+from jax.experimental import pallas as pl
+from jax.experimental.pallas import tpu as pltpu
 from jax.sharding import PartitionSpec as P
 
 BLOCK = 256
@@ -71,6 +73,7 @@
 
 CTX = ("zh", "zl", "core")
 SWAP = ((0, 1), (1, 0))
+SLOTS = 8
 
 
 def swap(array, axis):
@@ -80,19 +83,6 @@
 def four(array, across):
     beside = swap(array, "core")
     return (array, beside, across, swap(across, "core"))
-
-
-def absolute(pieces):
-    zl = lax.axis_index("zl")
-    core = lax.axis_index("core")
-    first, second, third, fourth = pieces
-    low = jnp.where(core == 0, first, second), jnp.where(core == 0, second, first)
-    high = jnp.where(core == 0, third, fourth), jnp.where(core == 0, fourth, third)
-    low = jnp.stack(low)
-    high = jnp.stack(high)
-    return jnp.concatenate(
-        [jnp.where(zl == 0, low, high), jnp.where(zl == 0, high, low)], axis=0
-    )
 
 
 def joined(first, second):
@@ -154,60 +144,152 @@
     return joined((jnp.zeros_like(before[0]), outside), before)[1]
 
 
-def route(expert_ids, route_weights, expert_count, capacity):
+def combine_map(expert_ids, route_weights, expert_count, capacity):
     group_size = expert_ids.shape[0]
-    quarter = capacity // 4
-    part = lax.axis_index("zl") * 2 + lax.axis_index("core")
     assigned = expert_ids.reshape(group_size * 2)
     onehot = (
         assigned[:, None] == lax.broadcasted_iota(jnp.int32, (group_size * 2, expert_count), 1)
     ).astype(jnp.int32)
     earlier_count = jnp.cumsum(onehot, axis=0) - onehot
-    slot = jnp.sum(earlier_count * onehot, axis=1)
-    ours = slot - part * quarter
-    place = jnp.where((ours >= 0) & (ours < quarter), assigned * quarter + ours, -1)
-
-    def matches(position, count):
-        return (
-            position[:, None] == lax.broadcasted_iota(jnp.int32, (group_size * 2, count), 1)
-        ).astype(jnp.float32)
-
-    dispatch = jnp.sum(
-        matches(place, expert_count * quarter).reshape(group_size, 2, -1), axis=1
+    position = jnp.sum((earlier_count + assigned[:, None] * capacity) * onehot, axis=1)
+    matches = (
+        position[:, None]
+        == lax.broadcasted_iota(jnp.int32, (group_size * 2, expert_count * capacity), 1)
+    ).astype(jnp.float32)
+    return jnp.sum(
+        (matches * route_weights.reshape(group_size * 2)[:, None]).reshape(group_size, 2, -1),
+        axis=1,
+    )
+
+
+def pack_kernel(part_ref, ids_ref, tokens_ref, out_ref, onehot_ref):
+    group_size = tokens_ref.shape[0]
+    row_count = out_ref.shape[0]
+    expert_count = row_count // (2 * SLOTS)
+
+    @pl.when(pl.program_id(0) == 0)
+    def _():
+        shape = (expert_count, group_size)
+        expert = lax.broadcasted_iota(jnp.int32, shape, 0)
+        named = (ids_ref[0:1, :] == expert) | (ids_ref[1:2, :] == expert)
+        named = jnp.where(named, 1.0, 0.0)
+        square = (group_size, group_size)
+        earlier = lax.broadcasted_iota(jnp.int32, square, 0) < lax.broadcasted_iota(
+            jnp.int32, square, 1
+        )
+        before = jnp.dot(
+            named.astype(jnp.bfloat16),
+            jnp.where(earlier, 1.0, 0.0).astype(jnp.bfloat16),
+            preferred_element_type=jnp.float32,
+        )
+        slot = jnp.where(named > 0.0, before, -1.0)
+        wide = (expert_count, row_count // expert_count, group_size)
+        slot = jnp.broadcast_to(slot[:, None, :], wide).reshape(row_count, group_size)
+        row = lax.broadcasted_iota(jnp.int32, (row_count, group_size), 0)
+        wanted = part_ref[0] * SLOTS + jnp.bitwise_and(row, SLOTS - 1)
+        onehot_ref[...] = jnp.where(slot == wanted.astype(jnp.float32), 1.0, 0.0).astype(
+            jnp.bfloat16
+        )
+
+    out_ref[...] = jnp.dot(
+        onehot_ref[...], tokens_ref[...], preferred_element_type=jnp.float32
     ).astype(jnp.bfloat16)
-    combine = jnp.sum(
-        (
-            matches(assigned * capacity + slot, expert_count * capacity)
-            * route_weights.reshape(group_size * 2)[:, None]
-        ).reshape(group_size, 2, -1),
-        axis=1,
-    )
-    return dispatch.reshape(group_size, expert_count, quarter), combine
-
-
-def packed_slots(moe_tokens, dispatch):
-    group_size, expert_count, rows = dispatch.shape
-    onehot = jnp.broadcast_to(dispatch[:, :, None, :], (group_size, expert_count, 2, rows))
-    packed = jnp.einsum("iehs,id->ehsd", onehot, moe_tokens, preferred_element_type=jnp.float32)
-    return packed.astype(jnp.bfloat16).reshape(2 * expert_count, rows, -1)
-
-
-def hidden_units(arrived, weights, hidden_count):
-    pieces = []
-    for weight in weights:
-        sums = lax.dot_general(
-            weight, arrived, (((0,), (1,)), ((), ())), preferred_element_type=jnp.float32
-        ).reshape(2, 2, hidden_count, -1)
-        acted = (jax.nn.silu(sums[:, 0]) * sums[:, 1]).astype(jnp.bfloat16)
-        pieces.extend((acted[0], acted[1]))
-    return absolute(pieces).reshape(4 * hidden_count, -1)
-
-
-def down_sums(hidden, extra, down):
+
+
+def packed_slots(moe_tokens, expert_ids, expert_count):
+    group_size, width = moe_tokens.shape
+    row_count = 2 * expert_count * SLOTS
+    steps = 2
+    part = (lax.axis_index("zl") * 2 + lax.axis_index("core")).astype(jnp.int32).reshape(1)
+    packed = pl.pallas_call(
+        pack_kernel,
+        grid=(steps,),
+        out_shape=jax.ShapeDtypeStruct((row_count, width), jnp.bfloat16),
+        in_specs=[
+            pl.BlockSpec(memory_space=pltpu.SMEM),
+            pl.BlockSpec((2, group_size), lambda i: (0, 0)),
+            pl.BlockSpec((group_size, width // steps), lambda i: (0, i)),
+        ],
+        out_specs=pl.BlockSpec((row_count, width // steps), lambda i: (0, i)),
+        scratch_shapes=[pltpu.VMEM((row_count, group_size), jnp.bfloat16)],
+        cost_estimate=pl.CostEstimate(
+            flops=2 * row_count * group_size * width,
+            bytes_accessed=2 * (row_count + group_size) * width,
+            transcendentals=0,
+        ),
+        name="pack",
+    )(part, expert_ids.T, moe_tokens)
+    return packed.reshape(2 * expert_count, SLOTS, width)
+
+
+def hidden_kernel(part_ref, slots_ref, head_ref, *refs):
+    pieces, (out_ref, slots, weights, slots_sem, sems) = refs[:8], refs[8:]
+    count = pieces[0].shape[0]
+    head = head_ref.shape[0]
+    copies = [pltpu.make_async_copy(slots_ref, slots, slots_sem)]
+    for i, piece in enumerate(pieces):
+        copies.append(
+            pltpu.make_async_copy(piece, weights.at[pl.ds(i * count, count)], sems.at[i])
+        )
+    for copy in copies:
+        copy.start()
+    out_ref[pl.ds(0, head), :] = head_ref[...]
+    copies[0].wait()
+    part = part_ref[0]
+    for first in range(0, 4, 2):
+        for copy in copies[1 + 2 * first : 1 + 2 * (first + 2)]:
+            copy.wait()
+        sums = [
+            lax.dot_general(
+                weights[pl.ds(2 * count * member, 2 * count), :],
+                slots[...],
+                (((1,), (1,)), ((), ())),
+                preferred_element_type=jnp.float32,
+            )
+            for member in range(first, first + 2)
+        ]
+        for i, both in enumerate(sums):
+            gate, up = both[:count], both[count:]
+            place = jnp.bitwise_xor(part, first + i) * count + head
+            hidden = gate / (1.0 + jnp.exp(-gate)) * up
+            out_ref[pl.ds(pl.multiple_of(place, 16), count), :] = hidden.astype(jnp.bfloat16)
+
+
+def ring_message(arrived, head, gates, ups):
+    count = gates[0].shape[1]
+    slot_count, width = arrived.shape
+    pieces = [weight.T for pair in zip(gates, ups) for weight in pair]
+    part = (lax.axis_index("zl") * 2 + lax.axis_index("core")).astype(jnp.int32).reshape(1)
+    anywhere = pl.BlockSpec(memory_space=pl.ANY)
+    return pl.pallas_call(
+        hidden_kernel,
+        out_shape=jax.ShapeDtypeStruct((head.shape[0] + 4 * count, slot_count), jnp.bfloat16),
+        in_specs=[
+            pl.BlockSpec(memory_space=pltpu.SMEM),
+            anywhere,
+            pl.BlockSpec(memory_space=pltpu.VMEM),
+            *[anywhere] * 8,
+        ],
+        out_specs=pl.BlockSpec(memory_space=pltpu.VMEM),
+        scratch_shapes=[
+            pltpu.VMEM((slot_count, width), jnp.bfloat16),
+            pltpu.VMEM((8 * count, width), jnp.bfloat16),
+            pltpu.SemaphoreType.DMA,
+            pltpu.SemaphoreType.DMA((8,)),
+        ],
+        cost_estimate=pl.CostEstimate(
+            flops=16 * count * slot_count * width,
+            bytes_accessed=2 * (8 * count + slot_count) * width,
+            transcendentals=4 * count * slot_count,
+        ),
+        name="hidden",
+    )(part, arrived, head, *pieces)
+
+
+def down_sums(message, head, down):
     place = lax.axis_index("zh")
     count = lax.axis_size("zh")
-    size = hidden.shape[0]
-    head = extra.shape[0]
+    size = message.shape[0] - head
     ahead = [(i, (i + 1) % count) for i in range(count)]
     behind = [(i, (i - 1) % count) for i in range(count)]
 
@@ -221,9 +303,9 @@
     def both(step, near):
         return product(-step, 0, near[0][head:]) + product(step, 0, near[1][head:])
 
-    forward = backward = jnp.concatenate([extra, hidden], axis=0)
+    forward = backward = message
     offsets, extras = [], []
-    total = product(0, 0, hidden)
+    total = product(0, 0, message[head:])
     last = count // 2
     for step in range(1, last):
         forward = lax.ppermute(forward, "zh", ahead)
@@ -263,12 +345,11 @@
     group_size = moe_tokens.shape[0]
     expert_count = lax.axis_size("exp") // 2
     capacity = min(group_size, 4 * group_size // expert_count)
-    rows = capacity // 4
-    hidden_count = gate_proj.shape[2]
+    rows = SLOTS
+    assert capacity == 4 * rows
     gate, up, down = gate_proj[0], up_proj[0], down_proj[0]
     gate_across = swap(gate, "zl")
-    dispatch, combine = route(expert_ids, route_weights, expert_count, capacity)
-    packed = packed_slots(moe_tokens, dispatch)
+    packed = packed_slots(moe_tokens, expert_ids, expert_count)
     packed, gate, up, down, seq_inputs, step_size = lax.optimization_barrier(
         (packed, gate, up, down, seq_inputs, step_size)
     )
@@ -277,31 +358,33 @@
     down_across = swap(down, "zl")
     gates = four(gate, gate_across)
     ups = four(up, up_across)
-    weights = [
-        jnp.concatenate([gates[r], ups[r], gates[r + 1], ups[r + 1]], axis=1) for r in (0, 2)
-    ]
     down_columns = jnp.concatenate(four(down, down_across), axis=1)
     local_mix, cumulative, block_ends, entering, final = mixer_prepare(
         seq_inputs, step_size, write_map, read_map, decay_log
     )
     group, before = group_state(jnp.sum(block_ends, axis=1), final)
-    hidden = hidden_units(arrived.reshape(2 * expert_count * rows, -1), weights, hidden_count)
-    state_part = state_rows(*group, hidden.shape[1])
-    sums, offsets, extras = down_sums(hidden, state_part, down_columns)
+    state_part = state_rows(*group, 2 * expert_count * rows)
+    head = state_part.shape[0]
+    message = ring_message(
+        arrived.reshape(2 * expert_count * rows, -1), state_part, gates, ups
+    )
+    sums, offsets, extras = down_sums(message, head, down_columns)
     width = down.shape[1]
     blocks = sums.reshape(2 * expert_count, rows, 4, width).transpose(2, 0, 1, 3)
     blocks = ordered(blocks.reshape(2, 2, 2 * expert_count, rows, width))
     blocks = blocks.transpose(2, 0, 1, 3, 4).reshape(8 * expert_count, rows, width)
-    blocks, *extras = lax.optimization_barrier((blocks, *extras))
+    blocks, expert_ids, route_weights, *extras = lax.optimization_barrier(
+        (blocks, expert_ids, route_weights, *extras)
+    )
     returned = lax.all_to_all(
         blocks, ("exp", "zl", "core"), split_axis=0, concat_axis=0, tiled=True
     )
-    head = state_part.shape[0]
     states = jnp.stack([message[:head] for message in extras])
     state_before = state_ahead(offsets, *read_rows(states, final.shape), before)
     mixer_output = mixer_finish(
         local_mix, cumulative, block_ends, entering, state_before, read_map, seq_inputs, skip_gain
     )
+    combine = combine_map(expert_ids, route_weights, expert_count, capacity)
     summed = jnp.sum(returned.reshape(expert_count, 2, capacity, width), axis=1)
     expert_output = jnp.dot(
         combine,

time: 210 us -> 206 us (0.981)
  waiting for transfers between devices: 69.5 us -> 41.9 us
  starting transfers between devices: 91.2 us -> 111 us
  Pallas kernels: 0 us -> 11 us
  other arithmetic: 17.7 us -> 8.26 us
  local copies, waits for them, and re-layouts: 15.8 us -> 20.4 us
  matrix products: 13.1 us -> 10.3 us
    ppermute x3, starting transfers between devices: 12.3 us -> 28.8 us  [down_sums(): backward = lax.ppermute(backward, 'zh', behind)]
    ppermute x11, waiting for transfers between devices: 26.5 us -> 12.9 us  [swap(): return lax.ppermute(array, axis, SWAP)]
    ppermute x3, waiting for transfers between devices: 11.8 us -> 0.01 us  [down_sums(): backward = lax.ppermute(backward, 'zh', behind)]
    pallas_call x0 -> x2, Pallas kernels: none -> 11 us  [the longest x1 7.88 us: ring_message(): pl.pallas_call(hidden_kernel, out_shape=jax.ShapeDtypeStruct((head.shape[...]
    dot_general x3 -> x0, matrix products: 6.72 us -> none  [the longest x2 4.61 us: hidden_units(): lax.dot_general(weight, arrived, (((0,), (1,)), ((), ())), preferred_elem...]
    concatenate x4 -> x1, other arithmetic: 6.63 us -> 0.61 us  [state_rows(): jnp.concatenate([high, flat - high, logs], axis=0).astype(jnp.bfloat16)]
    ppermute x3, waiting for transfers between devices: 14.6 us -> 9.72 us  [down_sums(): forward = lax.ppermute(forward, 'zh', ahead)]
    all_to_all x1, waiting for transfers between devices: 0.01 us -> 4.11 us  [layer(): lax.all_to_all(packed, 'exp', split_axis=0, concat_axis=0, tiled=True)]
  transfers between devices with their start and end apart: 21 -> 21, of which waited for: 9 -> 7; matrix products, arithmetic and copies ran while one was open for 18% -> 15% of each run, Pallas kernels for 0% -> 4%
where the time goes in v2:
time: 206 us; the launch traced here: 205 us
  starting transfers between devices  111 us (54%)
  waiting for transfers between devices  41.9 us (20%)
  local copies, waits for them, and re-layouts  20.4 us (10%)
  Pallas kernels  11 us (5%)
  matrix products  10.3 us (5%)
  other arithmetic  8.26 us (4%)
    ppermute x11, starting transfers between devices, swap(): return lax.ppermute(array, axis, SWAP)  43.2 us
    ppermute x3, starting transfers between devices, down_sums(): backward = lax.ppermute(backward, 'zh', behind)  28.8 us
    all_to_all x1, starting transfers between devices, layer(): lax.all_to_all(blocks, ('exp', 'zl', 'core'), split_axis=0, concat_axis=0...  19.2 us
    ppermute x11, waiting for transfers between devices, swap(): return lax.ppermute(array, axis, SWAP)  12.9 us
    all_to_all x1, waiting for transfers between devices, layer(): lax.all_to_all(blocks, ('exp', 'zl', 'core'), split_axis=0, concat_axis=0...  12.8 us
    unnamed x49, local copies, waits for them, and re-layouts  11.9 us
    ppermute x3, waiting for transfers between devices, down_sums(): forward = lax.ppermute(forward, 'zh', ahead)  9.72 us
    ppermute x1, starting transfers between devices, down_sums(): backward = lax.ppermute(backward[half:], 'zh', behind)  8.4 us
  transfers between devices with their start and end apart: 21, of which 7 were waited for; matrix products, arithmetic and copies ran while one was open for 15% of the time, Pallas kernels for 4%

profile of v2, /device:TPU:1, one launch (start us, length us, event | category | flops | bytes accessed | tf_op | source)
XLA Modules:
  0.0 204.7 jit_solution(14120031567516392022)
XLA Ops:
  0.6 3.1 %pack.1 = bf16[256,4096]{1,0:T(8,128)(2,1)} custom-call(s32[1]{0:T(128)} %bitcast.part_ref, s32[2,128]{1,0:T(2,128)} %bitcast.160, bf16[128,4096]{1,0:T(8,128)(2,1)} %tokens_ref.1), custom_call_target="tpu_custom_call" | custom-call | flops 268435456 | bytes 3145728 | tf_op jit(solution)/shard_map/pack/pallas_call | solution.py:204
  3.8 4.8 %collective-permute-start.5 = (bf16[4096,112]{0,1:T(8,128)(2,1)}, bf16[4096,112]{0,1:T(8,128)(2,1)}, u32[]{:S(2)}, u32[]{:S(2)}) collective-permute-start(bf16[4096,112]{0,1:T(8,128)(2,1)} %bitcast.137), channel_id=1, source_target_pairs={{0,64},{64,0},{1,65},{65,1},{2,66},{66,2},{3,67},{67,3},{4,68},{68... | collective-permute-start | bytes 2752520 | tf_op jit(solution)/shard_map/ppermute | solution.py:80
  8.6 13.1 %collective-permute-start.3 = (bf16[4096,112]{0,1:T(8,128)(2,1)}, bf16[4096,112]{0,1:T(8,128)(2,1)}, u32[]{:S(2)}, u32[]{:S(2)}) collective-permute-start(bf16[4096,112]{0,1:T(8,128)(2,1)} %bitcast.138), channel_id=1, source_target_pairs={{0,32},{32,0},{1,33},{33,1},{2,34},{34,2},{3,35},{35,3},{4,36},{36... | collective-permute-start | bytes 2752520 | tf_op jit(solution)/shard_map/ppermute | solution.py:80
  21.7 3.6 %collective-permute-start.4 = (bf16[4096,112]{0,1:T(8,128)(2,1)}, bf16[4096,112]{0,1:T(8,128)(2,1)}, u32[]{:S(2)}, u32[]{:S(2)}) collective-permute-start(bf16[4096,112]{0,1:T(8,128)(2,1)} %bitcast.134), channel_id=1, source_target_pairs={{0,64},{64,0},{1,65},{65,1},{2,66},{66,2},{3,67},{67,3},{4,68},{68... | collective-permute-start | bytes 2752520 | tf_op jit(solution)/shard_map/ppermute | solution.py:80
  27.5 2.4 %reduce-window.14 = f32[4,2,2,128]{3,2,1,0:T(2,128)S(1)} reduce-window(f32[4,2,2,128]{3,2,1,0:T(2,128)S(1)} %reshape.371, f32[]{:T(128)} %constant.112.clone.1), window={size=1x1x1x128 pad=0_0x0_0x0_0x127_0}, to_apply=%region_0.0 | reduce-window | flops 260096 | bytes 16388 | tf_op jit(solution)/shard_map/reduce-window
  33.6 2.3 %collective-permute-start = (f32[4,1025]{1,0:T(4,128)S(1)}, f32[4,1025]{1,0:T(4,128)S(1)}, u32[]{:S(2)}, u32[]{:S(2)}) collective-permute-start(f32[4,1025]{1,0:T(4,128)S(1)} %pad_maximum_fusion.1), channel_id=1, source_target_pairs={{0,32},{32,0},{1,33},{33,1},{2,34},{34,2},{3,35},{35,3},{4,36},{36... | collective-permute-start | bytes 49208 | tf_op jit(solution)/shard_map/ppermute | solution.py:80
  35.9 4.0 %all-to-all-start = ((bf16[32,8,4096]{2,1,0:T(8,128)(2,1)}), bf16[32,8,4096]{2,1,0:T(8,128)(2,1)S(1)}, u32[]{:S(2)}, u32[]{:S(2)}) async-start(bf16[32,8,4096]{2,1,0:T(8,128)(2,1)} %bitcast.130), calls=%async_computation | async-start | bytes 4194304 | tf_op jit(solution)/shard_map/all_to_all | solution.py:356
  48.8 2.4 %collective-permute-done.1 = f32[4,1025]{1,0:T(4,128)S(1)} collective-permute-done((f32[4,1025]{1,0:T(4,128)S(1)}, f32[4,1025]{1,0:T(4,128)S(1)}, u32[]{:S(2)}, u32[]{:S(2)}) %collective-permute-start.1) | collective-permute-done | bytes 16432 | tf_op jit(solution)/shard_map/ppermute | solution.py:80
  54.3 4.1 %collective-permute-start.2 = (bf16[4096,112]{0,1:T(8,128)(2,1)S(1)}, bf16[4096,112]{0,1:T(8,128)(2,1)S(1)}, u32[]{:S(2)}, u32[]{:S(2)}) collective-permute-start(bf16[4096,112]{0,1:T(8,128)(2,1)S(1)} %bitcast.136), channel_id=1, source_target_pairs={{0,32},{32,0},{1,33},{33,1},{2,34},{34,2},{3,35},{35,3},{4,36},{36... | collective-permute-start | bytes 2752520 | tf_op jit(solution)/shard_map/ppermute | solution.py:80
  60.3 2.4 %collective-permute-start.6 = (bf16[4096,112]{0,1:T(8,128)(2,1)}, bf16[4096,112]{0,1:T(8,128)(2,1)}, u32[]{:S(2)}, u32[]{:S(2)}) collective-permute-start(bf16[4096,112]{0,1:T(8,128)(2,1)} %collective-permute-done.4), channel_id=1, source_target_pairs={{0,32},{32,0},{1,33},{33,1},{2,34},{34,2},{3,35},{35,3},{4,36},{36... | collective-permute-start | bytes 2752520 | tf_op jit(solution)/shard_map/ppermute | solution.py:80
  62.7 10.5 %collective-permute-done.9 = bf16[3584,128]{1,0:T(8,128)(2,1)} collective-permute-done((bf16[3584,128]{1,0:T(8,128)(2,1)}, bf16[3584,128]{1,0:T(8,128)(2,1)}, u32[]{:S(2)}, u32[]{:S(2)}) %collective-permute-start.9) | collective-permute-done | bytes 917536 | tf_op jit(solution)/shard_map/ppermute | solution.py:80
  73.2 4.9 %collective-permute-start.10 = (bf16[3584,128]{1,0:T(8,128)(2,1)}, bf16[3584,128]{1,0:T(8,128)(2,1)}, u32[]{:S(2)}, u32[]{:S(2)}) collective-permute-start(bf16[3584,128]{1,0:T(8,128)(2,1)} %collective-permute-done.9), channel_id=1, source_target_pairs={{0,32},{32,0},{1,33},{33,1},{2,34},{34,2},{3,35},{35,3},{4,36},{36... | collective-permute-start | bytes 2752520 | tf_op jit(solution)/shard_map/ppermute | solution.py:80
  78.1 2.2 %constant_dynamic-update-slice_fusion.2 = bf16[3584,512]{1,0:T(8,128)(2,1)} fusion(bf16[3584,512]{1,0:T(8,128)(2,1)} %constant_dynamic-update-slice_fusion.3, bf16[3584,128]{1,0:T(8,128)(2,1)} %collective-permute-done.8), kind=kLoop, calls=%fused_computation.71 | loop fusion | bytes 1835008
  80.4 2.2 %constant_dynamic-update-slice_fusion.1 = bf16[3584,512]{1,0:T(8,128)(2,1)} fusion(bf16[3584,512]{1,0:T(8,128)(2,1)} %constant_dynamic-update-slice_fusion.2, bf16[3584,128]{1,0:T(8,128)(2,1)} %collective-permute-done.9), kind=kLoop, calls=%fused_computation.70 | loop fusion | bytes 1835008
  84.5 4.1 %all-to-all-done = bf16[32,8,4096]{2,1,0:T(8,128)(2,1)S(1)} async-done(((bf16[32,8,4096]{2,1,0:T(8,128)(2,1)}), bf16[32,8,4096]{2,1,0:T(8,128)(2,1)S(1)}, u32[]{:S(2)}, u32[]{:S(2)}) %all-to-all-start) | async-done | bytes 2097184 | tf_op jit(solution)/shard_map/all_to_all | solution.py:356
  89.9 7.9 %hidden.1 = bf16[496,256]{1,0:T(8,128)(2,1)} custom-call(s32[1]{0:T(128)} %bitcast.part_ref, bf16[256,4096]{1,0:T(8,128)(2,1)} %bitcast.129, bf16[48,256]{1,0:T(8,128)(2,1)} %pad_maximum_fusion.head_ref, bf16[112,4096]{1,0:T(8,128)(2,1)} %bitcast.135, bf16[112,4096]{1,0:T(8,128)(2,1)} %bitcast.139, bf16[112,4096]{1,0:T(8,128)(2,1)} %bitcast.140, ...), custom_call_target="tpu_custom_call" | custom-call | flops 1879048192 | bytes 9437184 | tf_op jit(solution)/shard_map/hidden/pallas_call | solution.py:264
  97.8 10.8 %collective-permute-start.12 = (bf16[496,256]{1,0:T(8,128)(2,1)}, bf16[496,256]{1,0:T(8,128)(2,1)S(1)}, u32[]{:S(2)}, u32[]{:S(2)}) collective-permute-start(bf16[496,256]{1,0:T(8,128)(2,1)} %hidden.1), channel_id=1, source_target_pairs={{0,896},{128,0},{256,128},{384,256},{512,384},{640,512},{768,640},... | collective-permute-start | bytes 761864 | tf_op jit(solution)/shard_map/ppermute | solution.py:312
  112.8 6.0 %collective-permute-start.14 = (bf16[496,256]{1,0:T(8,128)(2,1)S(1)}, bf16[496,256]{1,0:T(8,128)(2,1)S(1)}, u32[]{:S(2)}, u32[]{:S(2)}) collective-permute-start(bf16[496,256]{1,0:T(8,128)(2,1)S(1)} %collective-permute-done.12), channel_id=1, source_target_pairs={{0,896},{128,0},{256,128},{384,256},{512,384},{640,512},{768,640},... | collective-permute-start | bytes 761864 | tf_op jit(solution)/shard_map/ppermute | solution.py:312
  123.8 12.0 %collective-permute-start.16 = (bf16[496,256]{1,0:T(8,128)(2,1)S(1)}, bf16[496,256]{1,0:T(8,128)(2,1)S(1)}, u32[]{:S(2)}, u32[]{:S(2)}) collective-permute-start(bf16[496,256]{1,0:T(8,128)(2,1)S(1)} %collective-permute-done.14), channel_id=1, source_target_pairs={{0,896},{128,0},{256,128},{384,256},{512,384},{640,512},{768,640},... | collective-permute-start | bytes 761864 | tf_op jit(solution)/shard_map/ppermute | solution.py:312
  139.8 9.4 %collective-permute-done.15 = bf16[496,256]{1,0:T(8,128)(2,1)S(1)} collective-permute-done((bf16[496,256]{1,0:T(8,128)(2,1)S(1)}, bf16[496,256]{1,0:T(8,128)(2,1)S(1)}, u32[]{:S(2)}, u32[]{:S(2)}) %collective-permute-start.15) | collective-permute-done | bytes 253984 | tf_op jit(solution)/shard_map/ppermute | solution.py:311
  151.1 8.4 %collective-permute-start.18 = (bf16[256,256]{1,0:T(8,128)(2,1)S(1)}, bf16[256,256]{1,0:T(8,128)(2,1)S(1)}, u32[]{:S(2)}, u32[]{:S(2)}) collective-permute-start(bf16[256,256]{1,0:T(8,128)(2,1)S(1)} %slice.132), channel_id=1, source_target_pairs={{0,896},{128,0},{256,128},{384,256},{512,384},{640,512},{768,640},... | collective-permute-start | bytes 393224 | tf_op jit(solution)/shard_map/ppermute | solution.py:318
  159.8 2.3 %collective-permute-done.17 = bf16[240,256]{1,0:T(8,128)(2,1)S(1)} collective-permute-done((bf16[240,256]{1,0:T(8,128)(2,1)S(1)}, bf16[240,256]{1,0:T(8,128)(2,1)S(1)}, u32[]{:S(2)}, u32[]{:S(2)}) %collective-permute-start.17) | collective-permute-done | bytes 122912 | tf_op jit(solution)/shard_map/ppermute | solution.py:317
  165.5 19.2 %all-to-all-start.1 = ((f32[128,8,128]{2,1,0:T(8,128)}), f32[128,8,128]{2,1,0:T(8,128)S(1)}, u32[]{:S(2)}, u32[]{:S(2)}) async-start(f32[128,8,128]{2,1,0:T(8,128)} %bitcast.31), calls=%async_computation.1 | async-start | bytes 1048576 | tf_op jit(solution)/shard_map/all_to_all | solution.py:379
  190.8 12.8 %all-to-all-done.1 = f32[128,8,128]{2,1,0:T(8,128)S(1)} async-done(((f32[128,8,128]{2,1,0:T(8,128)}), f32[128,8,128]{2,1,0:T(8,128)S(1)}, u32[]{:S(2)}, u32[]{:S(2)}) %all-to-all-start.1) | async-done | bytes 524320 | tf_op jit(solution)/shard_map/all_to_all | solution.py:379
  (180 shorter events, 48.3 us)
Async XLA Ops:
  0.6 31.8 %copy-start.11 = (bf16[16,512]{1,0:T(8,128)(2,1)S(1)}, bf16[16,512]{1,0:T(8,128)(2,1)}, u32[]{:S(2)}) copy-start(bf16[16,512]{1,0:T(8,128)(2,1)} %param.17) | copy-start | bytes 49156
  3.8 50.5 %collective-permute-start.5 = (bf16[4096,112]{0,1:T(8,128)(2,1)}, bf16[4096,112]{0,1:T(8,128)(2,1)}, u32[]{:S(2)}, u32[]{:S(2)}) collective-permute-start(bf16[4096,112]{0,1:T(8,128)(2,1)} %bitcast.137), channel_id=1, source_target_pairs={{0,64},{64,0},{1,65},{65,1},{2,66},{66,2},{3,67},{67,3},{4,68},{68... | collective-permute-start | bytes 2752520 | tf_op jit(solution)/shard_map/ppermute | solution.py:80
  8.6 74.0 %collective-permute-start.3 = (bf16[4096,112]{0,1:T(8,128)(2,1)}, bf16[4096,112]{0,1:T(8,128)(2,1)}, u32[]{:S(2)}, u32[]{:S(2)}) collective-permute-start(bf16[4096,112]{0,1:T(8,128)(2,1)} %bitcast.138), channel_id=1, source_target_pairs={{0,32},{32,0},{1,33},{33,1},{2,34},{34,2},{3,35},{35,3},{4,36},{36... | collective-permute-start | bytes 2752520 | tf_op jit(solution)/shard_map/ppermute | solution.py:80
  21.7 36.7 %collective-permute-start.4 = (bf16[4096,112]{0,1:T(8,128)(2,1)}, bf16[4096,112]{0,1:T(8,128)(2,1)}, u32[]{:S(2)}, u32[]{:S(2)}) collective-permute-start(bf16[4096,112]{0,1:T(8,128)(2,1)} %bitcast.134), channel_id=1, source_target_pairs={{0,64},{64,0},{1,65},{65,1},{2,66},{66,2},{3,67},{67,3},{4,68},{68... | collective-permute-start | bytes 2752520 | tf_op jit(solution)/shard_map/ppermute | solution.py:80
  33.6 11.9 %collective-permute-start = (f32[4,1025]{1,0:T(4,128)S(1)}, f32[4,1025]{1,0:T(4,128)S(1)}, u32[]{:S(2)}, u32[]{:S(2)}) collective-permute-start(f32[4,1025]{1,0:T(4,128)S(1)} %pad_maximum_fusion.1), channel_id=1, source_target_pairs={{0,32},{32,0},{1,33},{33,1},{2,34},{34,2},{3,35},{35,3},{4,36},{36... | collective-permute-start | bytes 49208 | tf_op jit(solution)/shard_map/ppermute | solution.py:80
  35.9 52.7 %all-to-all-start = ((bf16[32,8,4096]{2,1,0:T(8,128)(2,1)}), bf16[32,8,4096]{2,1,0:T(8,128)(2,1)S(1)}, u32[]{:S(2)}, u32[]{:S(2)}) async-start(bf16[32,8,4096]{2,1,0:T(8,128)(2,1)} %bitcast.130), calls=%async_computation | async-start | bytes 4194304 | tf_op jit(solution)/shard_map/all_to_all | solution.py:356
  40.0 20.3 %collective-permute-start.8 = (bf16[3584,128]{1,0:T(8,128)(2,1)}, bf16[3584,128]{1,0:T(8,128)(2,1)}, u32[]{:S(2)}, u32[]{:S(2)}) collective-permute-start(bf16[3584,128]{1,0:T(8,128)(2,1)} %bitcast.142), channel_id=1, source_target_pairs={{0,32},{32,0},{1,33},{33,1},{2,34},{34,2},{3,35},{35,3},{4,36},{36... | collective-permute-start | bytes 2752520 | tf_op jit(solution)/shard_map/ppermute | solution.py:80
  46.2 5.1 %collective-permute-start.1 = (f32[4,1025]{1,0:T(4,128)S(1)}, f32[4,1025]{1,0:T(4,128)S(1)}, u32[]{:S(2)}, u32[]{:S(2)}) collective-permute-start(f32[4,1025]{1,0:T(4,128)S(1)} %pad_maximum_fusion.2), channel_id=1, source_target_pairs={{0,64},{64,0},{1,65},{65,1},{2,66},{66,2},{3,67},{67,3},{4,68},{68... | collective-permute-start | bytes 49208 | tf_op jit(solution)/shard_map/ppermute | solution.py:80
  51.3 21.9 %collective-permute-start.9 = (bf16[3584,128]{1,0:T(8,128)(2,1)}, bf16[3584,128]{1,0:T(8,128)(2,1)}, u32[]{:S(2)}, u32[]{:S(2)}) collective-permute-start(bf16[3584,128]{1,0:T(8,128)(2,1)} %bitcast.144), channel_id=1, source_target_pairs={{0,64},{64,0},{1,65},{65,1},{2,66},{66,2},{3,67},{67,3},{4,68},{68... | collective-permute-start | bytes 2752520 | tf_op jit(solution)/shard_map/ppermute | solution.py:80
  54.3 28.3 %collective-permute-start.2 = (bf16[4096,112]{0,1:T(8,128)(2,1)S(1)}, bf16[4096,112]{0,1:T(8,128)(2,1)S(1)}, u32[]{:S(2)}, u32[]{:S(2)}) collective-permute-start(bf16[4096,112]{0,1:T(8,128)(2,1)S(1)} %bitcast.136), channel_id=1, source_target_pairs={{0,32},{32,0},{1,33},{33,1},{2,34},{34,2},{3,35},{35,3},{4,36},{36... | collective-permute-start | bytes 2752520 | tf_op jit(solution)/shard_map/ppermute | solution.py:80
  58.4 24.2 %collective-permute-start.7 = (bf16[4096,112]{0,1:T(8,128)(2,1)}, bf16[4096,112]{0,1:T(8,128)(2,1)S(1)}, u32[]{:S(2)}, u32[]{:S(2)}) collective-permute-start(bf16[4096,112]{0,1:T(8,128)(2,1)} %collective-permute-done.5), channel_id=1, source_target_pairs={{0,32},{32,0},{1,33},{33,1},{2,34},{34,2},{3,35},{35,3},{4,36},{36... | collective-permute-start | bytes 2752520 | tf_op jit(solution)/shard_map/ppermute | solution.py:80
  60.3 24.2 %collective-permute-start.6 = (bf16[4096,112]{0,1:T(8,128)(2,1)}, bf16[4096,112]{0,1:T(8,128)(2,1)}, u32[]{:S(2)}, u32[]{:S(2)}) collective-permute-start(bf16[4096,112]{0,1:T(8,128)(2,1)} %collective-permute-done.4), channel_id=1, source_target_pairs={{0,32},{32,0},{1,33},{33,1},{2,34},{34,2},{3,35},{35,3},{4,36},{36... | collective-permute-start | bytes 2752520 | tf_op jit(solution)/shard_map/ppermute | solution.py:80
  73.2 37.4 %collective-permute-start.10 = (bf16[3584,128]{1,0:T(8,128)(2,1)}, bf16[3584,128]{1,0:T(8,128)(2,1)}, u32[]{:S(2)}, u32[]{:S(2)}) collective-permute-start(bf16[3584,128]{1,0:T(8,128)(2,1)} %collective-permute-done.9), channel_id=1, source_target_pairs={{0,32},{32,0},{1,33},{33,1},{2,34},{34,2},{3,35},{35,3},{4,36},{36... | collective-permute-start | bytes 2752520 | tf_op jit(solution)/shard_map/ppermute | solution.py:80
  97.8 41.6 %copy-start.2 = (bf16[496,256]{1,0:T(8,128)(2,1)S(1)}, bf16[496,256]{1,0:T(8,128)(2,1)}, u32[]{:S(2)}) copy-start(bf16[496,256]{1,0:T(8,128)(2,1)} %hidden.1) | copy-start | bytes 761860
  97.8 15.0 %collective-permute-start.12 = (bf16[496,256]{1,0:T(8,128)(2,1)}, bf16[496,256]{1,0:T(8,128)(2,1)S(1)}, u32[]{:S(2)}, u32[]{:S(2)}) collective-permute-start(bf16[496,256]{1,0:T(8,128)(2,1)} %hidden.1), channel_id=1, source_target_pairs={{0,896},{128,0},{256,128},{384,256},{512,384},{640,512},{768,640},... | collective-permute-start | bytes 761864 | tf_op jit(solution)/shard_map/ppermute | solution.py:312
  108.6 10.5 %collective-permute-start.11 = (bf16[496,256]{1,0:T(8,128)(2,1)}, bf16[496,256]{1,0:T(8,128)(2,1)S(1)}, u32[]{:S(2)}, u32[]{:S(2)}) collective-permute-start(bf16[496,256]{1,0:T(8,128)(2,1)} %hidden.1), channel_id=1, source_target_pairs={{0,128},{128,256},{256,384},{384,512},{512,640},{640,768},{768,896... | collective-permute-start | bytes 761864 | tf_op jit(solution)/shard_map/ppermute | solution.py:311
  112.8 10.9 %collective-permute-start.14 = (bf16[496,256]{1,0:T(8,128)(2,1)S(1)}, bf16[496,256]{1,0:T(8,128)(2,1)S(1)}, u32[]{:S(2)}, u32[]{:S(2)}) collective-permute-start(bf16[496,256]{1,0:T(8,128)(2,1)S(1)} %collective-permute-done.12), channel_id=1, source_target_pairs={{0,896},{128,0},{256,128},{384,256},{512,384},{640,512},{768,640},... | collective-permute-start | bytes 761864 | tf_op jit(solution)/shard_map/ppermute | solution.py:312
  119.1 18.0 %collective-permute-start.13 = (bf16[496,256]{1,0:T(8,128)(2,1)S(1)}, bf16[496,256]{1,0:T(8,128)(2,1)S(1)}, u32[]{:S(2)}, u32[]{:S(2)}) collective-permute-start(bf16[496,256]{1,0:T(8,128)(2,1)S(1)} %collective-permute-done.11), channel_id=1, source_target_pairs={{0,128},{128,256},{256,384},{384,512},{512,640},{640,768},{768,896... | collective-permute-start | bytes 761864 | tf_op jit(solution)/shard_map/ppermute | solution.py:311
  123.8 38.7 %copy-start.8 = (bf16[496,256]{1,0:T(8,128)(2,1)}, bf16[496,256]{1,0:T(8,128)(2,1)S(1)}, u32[]{:S(2)}) copy-start(bf16[496,256]{1,0:T(8,128)(2,1)S(1)} %collective-permute-done.14) | copy-start | bytes 761860
  123.8 27.3 %collective-permute-start.16 = (bf16[496,256]{1,0:T(8,128)(2,1)S(1)}, bf16[496,256]{1,0:T(8,128)(2,1)S(1)}, u32[]{:S(2)}, u32[]{:S(2)}) collective-permute-start(bf16[496,256]{1,0:T(8,128)(2,1)S(1)} %collective-permute-done.14), channel_id=1, source_target_pairs={{0,896},{128,0},{256,128},{384,256},{512,384},{640,512},{768,640},... | collective-permute-start | bytes 761864 | tf_op jit(solution)/shard_map/ppermute | solution.py:312
  137.2 12.0 %collective-permute-start.15 = (bf16[496,256]{1,0:T(8,128)(2,1)S(1)}, bf16[496,256]{1,0:T(8,128)(2,1)S(1)}, u32[]{:S(2)}, u32[]{:S(2)}) collective-permute-start(bf16[496,256]{1,0:T(8,128)(2,1)S(1)} %collective-permute-done.13), channel_id=1, source_target_pairs={{0,128},{128,256},{256,384},{384,512},{512,640},{640,768},{768,896... | collective-permute-start | bytes 761864 | tf_op jit(solution)/shard_map/ppermute | solution.py:311
  149.1 13.0 %collective-permute-start.17 = (bf16[240,256]{1,0:T(8,128)(2,1)S(1)}, bf16[240,256]{1,0:T(8,128)(2,1)S(1)}, u32[]{:S(2)}, u32[]{:S(2)}) collective-permute-start(bf16[240,256]{1,0:T(8,128)(2,1)S(1)} %slice.130), channel_id=1, source_target_pairs={{0,128},{128,256},{256,384},{384,512},{512,640},{640,768},{768,896... | collective-permute-start | bytes 368648 | tf_op jit(solution)/shard_map/ppermute | solution.py:317
  151.1 11.3 %collective-permute-start.18 = (bf16[256,256]{1,0:T(8,128)(2,1)S(1)}, bf16[256,256]{1,0:T(8,128)(2,1)S(1)}, u32[]{:S(2)}, u32[]{:S(2)}) collective-permute-start(bf16[256,256]{1,0:T(8,128)(2,1)S(1)} %slice.132), channel_id=1, source_target_pairs={{0,896},{128,0},{256,128},{384,256},{512,384},{640,512},{768,640},... | collective-permute-start | bytes 393224 | tf_op jit(solution)/shard_map/ppermute | solution.py:318
  165.5 38.1 %all-to-all-start.1 = ((f32[128,8,128]{2,1,0:T(8,128)}), f32[128,8,128]{2,1,0:T(8,128)S(1)}, u32[]{:S(2)}, u32[]{:S(2)}) async-start(f32[128,8,128]{2,1,0:T(8,128)} %bitcast.31), calls=%async_computation.1 | async-start | bytes 1048576 | tf_op jit(solution)/shard_map/all_to_all | solution.py:379
  (15 other events, 203.2 us)

commit v3 on v2

--- a/solution.py
+++ b/solution.py
@@ -135,7 +135,8 @@
 def state_ahead(offsets, logs, states, before):
     place = lax.axis_index("zh")
     count = lax.axis_size("zh")
-    source = (place + jnp.array([o + count for o in offsets], jnp.int32)) % count
+    sign = 1 - 2 * lax.axis_index("core")
+    source = jnp.bitwise_and(place + sign * jnp.array(offsets, jnp.int32) + count, count - 1)
     earlier = source < place
     between = (source[None, :] > source[:, None]) & earlier[None, :]
     span = jnp.sum(jnp.where(between[:, :, None], logs[None], 0.0), axis=1)
@@ -286,40 +287,57 @@
     )(part, arrived, head, *pieces)
 
 
-def down_sums(message, head, down):
+def down_sums(message, head, downs):
     place = lax.axis_index("zh")
     count = lax.axis_size("zh")
     size = message.shape[0] - head
-    ahead = [(i, (i + 1) % count) for i in range(count)]
-    behind = [(i, (i - 1) % count) for i in range(count)]
+    sign = 1 - 2 * lax.axis_index("core")
+
+    def pairs(way):
+        steps = (way, -way)
+        return [
+            (2 * i + core, 2 * ((i + steps[core]) % count) + core)
+            for i in range(count)
+            for core in range(2)
+        ]
+
+    def move(array, way):
+        return lax.ppermute(array, ("zh", "core"), pairs(way))
 
     def product(offset, first, shard):
-        start = (place + (offset + count)) % count * size + first
-        rows = lax.dynamic_slice_in_dim(down, start, shard.shape[0], 0)
-        return lax.dot_general(
-            shard, rows, (((0,), (0,)), ((), ())), preferred_element_type=jnp.float32
-        )
-
-    def both(step, near):
-        return product(-step, 0, near[0][head:]) + product(step, 0, near[1][head:])
-
-    forward = backward = message
-    offsets, extras = [], []
+        start = jnp.bitwise_and(place + sign * offset + count, count - 1) * size + first
+        return [
+            lax.dot_general(
+                shard,
+                lax.dynamic_slice_in_dim(down, start, shard.shape[0], 0),
+                (((0,), (0,)), ((), ())),
+                preferred_element_type=jnp.float32,
+            )
+            for down in downs
+        ]
+
+    def added(*parts):
+        return [sum(part[1:], part[0]) for part in zip(*parts)]
+
+    first = second = message
+    offsets, received = [], []
     total = product(0, 0, message[head:])
     last = count // 2
     for step in range(1, last):
-        forward = lax.ppermute(forward, "zh", ahead)
-        backward = lax.ppermute(backward, "zh", behind)
+        first = move(first, 1)
+        second = move(second, -1)
         offsets += [-step, step]
-        extras += [forward, backward]
-        total = total + both(step, (forward, backward))
+        received += [first, second]
+        total = added(total, product(-step, 0, first[head:]), product(step, 0, second[head:]))
     half = (size + head) // 32 * 16
-    forward = lax.ppermute(forward[:half], "zh", ahead)
-    backward = lax.ppermute(backward[half:], "zh", behind)
+    first = move(first[:half], 1)
+    second = move(second[half:], -1)
     offsets.append(-last)
-    extras.append(forward)
-    total = total + product(-last, 0, forward[head:]) + product(last, half - head, backward)
-    return total, offsets, extras
+    received.append(first)
+    total = added(
+        total, product(-last, 0, first[head:]), product(last, half - head, second)
+    )
+    return total, offsets, received
 
 
 def ordered(blocks):
@@ -358,7 +376,9 @@
     down_across = swap(down, "zl")
     gates = four(gate, gate_across)
     ups = four(up, up_across)
-    down_columns = jnp.concatenate(four(down, down_across), axis=1)
+    downs = four(down, down_across)
+    near = jnp.concatenate(downs[:2], axis=1)
+    downs = near, jnp.concatenate(downs[2:], axis=1)
     local_mix, cumulative, block_ends, entering, final = mixer_prepare(
         seq_inputs, step_size, write_map, read_map, decay_log
     )
@@ -368,10 +388,12 @@
     message = ring_message(
         arrived.reshape(2 * expert_count * rows, -1), state_part, gates, ups
     )
-    sums, offsets, extras = down_sums(message, head, down_columns)
+    sums, offsets, extras = down_sums(message, head, downs)
     width = down.shape[1]
-    blocks = sums.reshape(2 * expert_count, rows, 4, width).transpose(2, 0, 1, 3)
-    blocks = ordered(blocks.reshape(2, 2, 2 * expert_count, rows, width))
+    blocks = jnp.stack(
+        [part.reshape(2 * expert_count, rows, 2, width).transpose(2, 0, 1, 3) for part in sums]
+    )
+    blocks = ordered(blocks)
     blocks = blocks.transpose(2, 0, 1, 3, 4).reshape(8 * expert_count, rows, width)
     blocks, expert_ids, route_weights, *extras = lax.optimization_barrier(
         (blocks, expert_ids, route_weights, *extras)

time: 206 us -> 213 us (1.034)
  waiting for transfers between devices: 41.9 us -> 48.2 us
  local copies, waits for them, and re-layouts: 20.4 us -> 17.9 us
    ppermute x11, waiting for transfers between devices: 12.9 us -> 18.1 us  [swap(): return lax.ppermute(array, axis, SWAP)]
    ppermute x8, starting transfers between devices: 44.8 us -> 39.7 us  [move(): return lax.ppermute(array, ('zh', 'core'), pairs(way))]
    all_to_all x1, starting transfers between devices: 19.2 us -> 24.1 us  [layer(): lax.all_to_all(blocks, ('exp', 'zl', 'core'), split_axis=0, concat_axis=0...]
    all_to_all x1, waiting for transfers between devices: 4.11 us -> 0.01 us  [layer(): lax.all_to_all(packed, 'exp', split_axis=0, concat_axis=0, tiled=True)]
    ppermute x8, waiting for transfers between devices: 12.1 us -> 15.9 us  [move(): return lax.ppermute(array, ('zh', 'core'), pairs(way))]
    unnamed x49 -> x76, local copies, waits for them, and re-layouts: 11.9 us -> 9.97 us
    dot_general x9 -> x18, matrix products: 5.85 us -> 7.76 us  [product(): lax.dot_general(shard, lax.dynamic_slice_in_dim(down, start, shard.shape[...]
  transfers between devices with their start and end apart: 21 -> 21, of which waited for: 7 -> 7; matrix products, arithmetic and copies ran while one was open for 15% -> 14% of each run, Pallas kernels for 4% -> 5%
where the time goes in v3:
time: 213 us; the launch traced here: 212 us
  starting transfers between devices  111 us (52%)
  waiting for transfers between devices  48.2 us (23%)
  local copies, waits for them, and re-layouts  17.9 us (8%)
  matrix products  11.4 us (5%)
  Pallas kernels  10.9 us (5%)
  other arithmetic  10.2 us (5%)
    ppermute x11, starting transfers between devices, swap(): return lax.ppermute(array, axis, SWAP)  43.4 us
    ppermute x8, starting transfers between devices, move(): return lax.ppermute(array, ('zh', 'core'), pairs(way))  39.7 us
    all_to_all x1, starting transfers between devices, layer(): lax.all_to_all(blocks, ('exp', 'zl', 'core'), split_axis=0, concat_axis=0...  24.1 us
    ppermute x11, waiting for transfers between devices, swap(): return lax.ppermute(array, axis, SWAP)  18.1 us
    ppermute x8, waiting for transfers between devices, move(): return lax.ppermute(array, ('zh', 'core'), pairs(way))  15.9 us
    all_to_all x1, waiting for transfers between devices, layer(): lax.all_to_all(blocks, ('exp', 'zl', 'core'), split_axis=0, concat_axis=0...  14.1 us
    unnamed x76, local copies, waits for them, and re-layouts  9.97 us
    pallas_call x1, Pallas kernels, ring_message(): pl.pallas_call(hidden_kernel, out_shape=jax.ShapeDtypeStruct((head.shape[...  7.9 us
  transfers between devices with their start and end apart: 21, of which 7 were waited for; matrix products, arithmetic and copies ran while one was open for 14% of the time, Pallas kernels for 5%

profile of v3, /device:TPU:1, one launch (start us, length us, event | category | flops | bytes accessed | tf_op | source)
XLA Modules:
  0.0 211.6 jit_solution(15306399843858935097)
XLA Ops:
  0.7 5.0 %collective-permute-start.4 = (bf16[4096,112]{0,1:T(8,128)(2,1)}, bf16[4096,112]{0,1:T(8,128)(2,1)}, u32[]{:S(2)}, u32[]{:S(2)}) collective-permute-start(bf16[4096,112]{0,1:T(8,128)(2,1)} %bitcast.141), channel_id=1, source_target_pairs={{0,64},{64,0},{1,65},{65,1},{2,66},{66,2},{3,67},{67,3},{4,68},{68... | collective-permute-start | bytes 2752520 | tf_op jit(solution)/shard_map/ppermute | solution.py:80
  5.6 3.0 %pack.1 = bf16[256,4096]{1,0:T(8,128)(2,1)} custom-call(s32[1]{0:T(128)} %bitcast.part_ref, s32[2,128]{1,0:T(2,128)} %bitcast.164, bf16[128,4096]{1,0:T(8,128)(2,1)} %tokens_ref.1), custom_call_target="tpu_custom_call" | custom-call | flops 268435456 | bytes 3145728 | tf_op jit(solution)/shard_map/pack/pallas_call | solution.py:205
  8.7 13.1 %collective-permute-start.3 = (bf16[4096,112]{0,1:T(8,128)(2,1)}, bf16[4096,112]{0,1:T(8,128)(2,1)}, u32[]{:S(2)}, u32[]{:S(2)}) collective-permute-start(bf16[4096,112]{0,1:T(8,128)(2,1)} %bitcast.4), channel_id=1, source_target_pairs={{0,32},{32,0},{1,33},{33,1},{2,34},{34,2},{3,35},{35,3},{4,36},{36... | collective-permute-start | bytes 2752520 | tf_op jit(solution)/shard_map/ppermute | solution.py:80
  21.8 3.6 %collective-permute-start.5 = (bf16[4096,112]{0,1:T(8,128)(2,1)}, bf16[4096,112]{0,1:T(8,128)(2,1)}, u32[]{:S(2)}, u32[]{:S(2)}) collective-permute-start(bf16[4096,112]{0,1:T(8,128)(2,1)} %bitcast.4), channel_id=1, source_target_pairs={{0,64},{64,0},{1,65},{65,1},{2,66},{66,2},{3,67},{67,3},{4,68},{68... | collective-permute-start | bytes 2752520 | tf_op jit(solution)/shard_map/ppermute | solution.py:80
  25.6 2.4 %reduce-window.14 = f32[4,2,2,128]{3,2,1,0:T(2,128)S(1)} reduce-window(f32[4,2,2,128]{3,2,1,0:T(2,128)S(1)} %reshape.371, f32[]{:T(128)} %constant.33.clone.1), window={size=1x1x1x128 pad=0_0x0_0x0_0x127_0}, to_apply=%region_0.0 | reduce-window | flops 260096 | bytes 16388 | tf_op jit(solution)/shard_map/reduce-window
  30.8 2.3 %collective-permute-start = (f32[4,1025]{1,0:T(4,128)S(1)}, f32[4,1025]{1,0:T(4,128)S(1)}, u32[]{:S(2)}, u32[]{:S(2)}) collective-permute-start(f32[4,1025]{1,0:T(4,128)S(1)} %pad_maximum_fusion.2), channel_id=1, source_target_pairs={{0,32},{32,0},{1,33},{33,1},{2,34},{34,2},{3,35},{35,3},{4,36},{36... | collective-permute-start | bytes 49208 | tf_op jit(solution)/shard_map/ppermute | solution.py:80
  33.1 4.0 %all-to-all-start = ((bf16[32,8,4096]{2,1,0:T(8,128)(2,1)}), bf16[32,8,4096]{2,1,0:T(8,128)(2,1)S(1)}, u32[]{:S(2)}, u32[]{:S(2)}) async-start(bf16[32,8,4096]{2,1,0:T(8,128)(2,1)} %bitcast.138), calls=%async_computation | async-start | bytes 4194304 | tf_op jit(solution)/shard_map/all_to_all | solution.py:374
  45.1 3.3 %collective-permute-start.1 = (f32[4,1025]{1,0:T(4,128)}, f32[4,1025]{1,0:T(4,128)S(1)}, u32[]{:S(2)}, u32[]{:S(2)}) collective-permute-start(f32[4,1025]{1,0:T(4,128)} %pad_maximum_fusion.3), channel_id=1, source_target_pairs={{0,64},{64,0},{1,65},{65,1},{2,66},{66,2},{3,67},{67,3},{4,68},{68... | collective-permute-start | bytes 49208 | tf_op jit(solution)/shard_map/ppermute | solution.py:80
  48.6 18.1 %collective-permute-done.1 = f32[4,1025]{1,0:T(4,128)S(1)} collective-permute-done((f32[4,1025]{1,0:T(4,128)}, f32[4,1025]{1,0:T(4,128)S(1)}, u32[]{:S(2)}, u32[]{:S(2)}) %collective-permute-start.1) | collective-permute-done | bytes 16432 | tf_op jit(solution)/shard_map/ppermute | solution.py:80
  66.7 5.3 %collective-permute-start.8 = (bf16[3584,128]{1,0:T(8,128)(2,1)}, bf16[3584,128]{1,0:T(8,128)(2,1)}, u32[]{:S(2)}, u32[]{:S(2)}) collective-permute-start(bf16[3584,128]{1,0:T(8,128)(2,1)} %bitcast.148), channel_id=1, source_target_pairs={{0,32},{32,0},{1,33},{33,1},{2,34},{34,2},{3,35},{35,3},{4,36},{36... | collective-permute-start | bytes 2752520 | tf_op jit(solution)/shard_map/ppermute | solution.py:80
  77.9 2.4 %collective-permute-start.6 = (bf16[4096,112]{0,1:T(8,128)(2,1)}, bf16[4096,112]{0,1:T(8,128)(2,1)S(1)}, u32[]{:S(2)}, u32[]{:S(2)}) collective-permute-start(bf16[4096,112]{0,1:T(8,128)(2,1)} %collective-permute-done.4), channel_id=1, source_target_pairs={{0,32},{32,0},{1,33},{33,1},{2,34},{34,2},{3,35},{35,3},{4,36},{36... | collective-permute-start | bytes 2752520 | tf_op jit(solution)/shard_map/ppermute | solution.py:80
  82.2 2.4 %collective-permute-start.18 = (bf16[3584,128]{1,0:T(8,128)(2,1)}, bf16[3584,128]{1,0:T(8,128)(2,1)}, u32[]{:S(2)}, u32[]{:S(2)}) collective-permute-start(bf16[3584,128]{1,0:T(8,128)(2,1)} %collective-permute-done.17), channel_id=1, source_target_pairs={{0,32},{32,0},{1,33},{33,1},{2,34},{34,2},{3,35},{35,3},{4,36},{36... | collective-permute-start | bytes 2752520 | tf_op jit(solution)/shard_map/ppermute | solution.py:80
  84.6 2.2 %constant_dynamic-update-slice_fusion.3 = bf16[3584,256]{1,0:T(8,128)(2,1)} fusion(bf16[3584,128]{1,0:T(8,128)(2,1)} %collective-permute-done.17), kind=kLoop, calls=%fused_computation.107 | loop fusion | bytes 1835008
  92.2 7.9 %hidden.1 = bf16[496,256]{1,0:T(8,128)(2,1)} custom-call(s32[1]{0:T(128)} %bitcast.part_ref, bf16[256,4096]{1,0:T(8,128)(2,1)} %bitcast.137, bf16[48,256]{1,0:T(8,128)(2,1)} %pad_maximum_fusion.1.head_ref, bf16[112,4096]{1,0:T(8,128)(2,1)} %bitcast.142, bf16[112,4096]{1,0:T(8,128)(2,1)} %bitcast.18.refs_1_, bf16[112,4096]{1,0:T(8,128)(2,1)} %bitcast.144, ...), custom_call_target="tpu_custom_call" | custom-call | flops 1879048192 | bytes 9437184 | tf_op jit(solution)/shard_map/hidden/pallas_call | solution.py:265
  100.1 2.6 %collective-permute-start.10 = (bf16[496,256]{1,0:T(8,128)(2,1)}, bf16[496,256]{1,0:T(8,128)(2,1)S(1)}, u32[]{:S(2)}, u32[]{:S(2)}) collective-permute-start(bf16[496,256]{1,0:T(8,128)(2,1)} %hidden.1), channel_id=1, source_target_pairs={{0,896},{32,160},{128,0},{160,288},{256,128},{288,416},{384,256},{... | collective-permute-start | bytes 761864 | tf_op jit(solution)/shard_map/ppermute | solution.py:305
  102.7 13.4 %collective-permute-start.9 = (bf16[496,256]{1,0:T(8,128)(2,1)}, bf16[496,256]{1,0:T(8,128)(2,1)S(1)}, u32[]{:S(2)}, u32[]{:S(2)}) collective-permute-start(bf16[496,256]{1,0:T(8,128)(2,1)} %hidden.1), channel_id=1, source_target_pairs={{0,128},{32,928},{128,256},{160,32},{256,384},{288,160},{384,512},... | collective-permute-start | bytes 761864 | tf_op jit(solution)/shard_map/ppermute | solution.py:305
  119.6 6.8 %collective-permute-done.9 = bf16[496,256]{1,0:T(8,128)(2,1)S(1)} collective-permute-done((bf16[496,256]{1,0:T(8,128)(2,1)}, bf16[496,256]{1,0:T(8,128)(2,1)S(1)}, u32[]{:S(2)}, u32[]{:S(2)}) %collective-permute-start.9) | collective-permute-done | bytes 253984 | tf_op jit(solution)/shard_map/ppermute | solution.py:305
  130.9 5.8 %collective-permute-start.11 = (bf16[496,256]{1,0:T(8,128)(2,1)S(1)}, bf16[496,256]{1,0:T(8,128)(2,1)S(1)}, u32[]{:S(2)}, u32[]{:S(2)}) collective-permute-start(bf16[496,256]{1,0:T(8,128)(2,1)S(1)} %collective-permute-done.9), channel_id=1, source_target_pairs={{0,128},{32,928},{128,256},{160,32},{256,384},{288,160},{384,512},... | collective-permute-start | bytes 761864 | tf_op jit(solution)/shard_map/ppermute | solution.py:305
  141.5 3.0 %collective-permute-done.11 = bf16[496,256]{1,0:T(8,128)(2,1)S(1)} collective-permute-done((bf16[496,256]{1,0:T(8,128)(2,1)S(1)}, bf16[496,256]{1,0:T(8,128)(2,1)S(1)}, u32[]{:S(2)}, u32[]{:S(2)}) %collective-permute-start.11) | collective-permute-done | bytes 253984 | tf_op jit(solution)/shard_map/ppermute | solution.py:305
  144.5 5.7 %collective-permute-start.13 = (bf16[496,256]{1,0:T(8,128)(2,1)S(1)}, bf16[496,256]{1,0:T(8,128)(2,1)S(1)}, u32[]{:S(2)}, u32[]{:S(2)}) collective-permute-start(bf16[496,256]{1,0:T(8,128)(2,1)S(1)} %collective-permute-done.11), channel_id=1, source_target_pairs={{0,128},{32,928},{128,256},{160,32},{256,384},{288,160},{384,512},... | collective-permute-start | bytes 761864 | tf_op jit(solution)/shard_map/ppermute | solution.py:305
  153.4 2.9 %collective-permute-done.13 = bf16[496,256]{1,0:T(8,128)(2,1)S(1)} collective-permute-done((bf16[496,256]{1,0:T(8,128)(2,1)S(1)}, bf16[496,256]{1,0:T(8,128)(2,1)S(1)}, u32[]{:S(2)}, u32[]{:S(2)}) %collective-permute-start.13) | collective-permute-done | bytes 253984 | tf_op jit(solution)/shard_map/ppermute | solution.py:305
  156.3 6.3 %collective-permute-start.15 = (bf16[240,256]{1,0:T(8,128)(2,1)S(1)}, bf16[240,256]{1,0:T(8,128)(2,1)S(1)}, u32[]{:S(2)}, u32[]{:S(2)}) collective-permute-start(bf16[240,256]{1,0:T(8,128)(2,1)S(1)} %slice.130), channel_id=1, source_target_pairs={{0,128},{32,928},{128,256},{160,32},{256,384},{288,160},{384,512},... | collective-permute-start | bytes 368648 | tf_op jit(solution)/shard_map/ppermute | solution.py:305
  167.6 24.1 %all-to-all-start.1 = ((f32[128,8,128]{2,1,0:T(8,128)}), f32[128,8,128]{2,1,0:T(8,128)S(1)}, u32[]{:S(2)}, u32[]{:S(2)}) async-start(f32[128,8,128]{2,1,0:T(8,128)} %bitcast.32), calls=%async_computation.1 | async-start | bytes 1048576 | tf_op jit(solution)/shard_map/all_to_all | solution.py:401
  196.4 14.1 %all-to-all-done.1 = f32[128,8,128]{2,1,0:T(8,128)S(1)} async-done(((f32[128,8,128]{2,1,0:T(8,128)}), f32[128,8,128]{2,1,0:T(8,128)S(1)}, u32[]{:S(2)}, u32[]{:S(2)}) %all-to-all-start.1) | async-done | bytes 524320 | tf_op jit(solution)/shard_map/all_to_all | solution.py:401
  (219 shorter events, 50.1 us)
Async XLA Ops:
  0.6 28.9 %copy-start.10 = (bf16[512,256]{1,0:T(8,128)(2,1)S(1)}, bf16[512,256]{1,0:T(8,128)(2,1)}, u32[]{:S(2)}) copy-start(bf16[512,256]{1,0:T(8,128)(2,1)} %param.15) | copy-start | bytes 786436
  0.7 75.3 %collective-permute-start.4 = (bf16[4096,112]{0,1:T(8,128)(2,1)}, bf16[4096,112]{0,1:T(8,128)(2,1)}, u32[]{:S(2)}, u32[]{:S(2)}) collective-permute-start(bf16[4096,112]{0,1:T(8,128)(2,1)} %bitcast.141), channel_id=1, source_target_pairs={{0,64},{64,0},{1,65},{65,1},{2,66},{66,2},{3,67},{67,3},{4,68},{68... | collective-permute-start | bytes 2752520 | tf_op jit(solution)/shard_map/ppermute | solution.py:80
  8.7 79.6 %collective-permute-start.3 = (bf16[4096,112]{0,1:T(8,128)(2,1)}, bf16[4096,112]{0,1:T(8,128)(2,1)}, u32[]{:S(2)}, u32[]{:S(2)}) collective-permute-start(bf16[4096,112]{0,1:T(8,128)(2,1)} %bitcast.4), channel_id=1, source_target_pairs={{0,32},{32,0},{1,33},{33,1},{2,34},{34,2},{3,35},{35,3},{4,36},{36... | collective-permute-start | bytes 2752520 | tf_op jit(solution)/shard_map/ppermute | solution.py:80
  21.8 56.1 %collective-permute-start.5 = (bf16[4096,112]{0,1:T(8,128)(2,1)}, bf16[4096,112]{0,1:T(8,128)(2,1)}, u32[]{:S(2)}, u32[]{:S(2)}) collective-permute-start(bf16[4096,112]{0,1:T(8,128)(2,1)} %bitcast.4), channel_id=1, source_target_pairs={{0,64},{64,0},{1,65},{65,1},{2,66},{66,2},{3,67},{67,3},{4,68},{68... | collective-permute-start | bytes 2752520 | tf_op jit(solution)/shard_map/ppermute | solution.py:80
  30.8 13.1 %collective-permute-start = (f32[4,1025]{1,0:T(4,128)S(1)}, f32[4,1025]{1,0:T(4,128)S(1)}, u32[]{:S(2)}, u32[]{:S(2)}) collective-permute-start(f32[4,1025]{1,0:T(4,128)S(1)} %pad_maximum_fusion.2), channel_id=1, source_target_pairs={{0,32},{32,0},{1,33},{33,1},{2,34},{34,2},{3,35},{35,3},{4,36},{36... | collective-permute-start | bytes 49208 | tf_op jit(solution)/shard_map/ppermute | solution.py:80
  33.1 57.7 %all-to-all-start = ((bf16[32,8,4096]{2,1,0:T(8,128)(2,1)}), bf16[32,8,4096]{2,1,0:T(8,128)(2,1)S(1)}, u32[]{:S(2)}, u32[]{:S(2)}) async-start(bf16[32,8,4096]{2,1,0:T(8,128)(2,1)} %bitcast.138), calls=%async_computation | async-start | bytes 4194304 | tf_op jit(solution)/shard_map/all_to_all | solution.py:374
  37.2 38.8 %copy-start.6 = (bf16[1,4096,112]{1,2,0:T(8,128)(2,1)S(1)}, bf16[1,4096,112]{1,2,0:T(8,128)(2,1)}, u32[]{:S(2)}) copy-start(bf16[1,4096,112]{1,2,0:T(8,128)(2,1)} %param.24) | copy-start | bytes 2752516
  37.2 43.1 %collective-permute-start.17 = (bf16[3584,128]{1,0:T(8,128)(2,1)}, bf16[3584,128]{1,0:T(8,128)(2,1)}, u32[]{:S(2)}, u32[]{:S(2)}) collective-permute-start(bf16[3584,128]{1,0:T(8,128)(2,1)} %bitcast.146), channel_id=1, source_target_pairs={{0,64},{64,0},{1,65},{65,1},{2,66},{66,2},{3,67},{67,3},{4,68},{68... | collective-permute-start | bytes 2752520 | tf_op jit(solution)/shard_map/ppermute | solution.py:80
  45.1 21.6 %collective-permute-start.1 = (f32[4,1025]{1,0:T(4,128)}, f32[4,1025]{1,0:T(4,128)S(1)}, u32[]{:S(2)}, u32[]{:S(2)}) collective-permute-start(f32[4,1025]{1,0:T(4,128)} %pad_maximum_fusion.3), channel_id=1, source_target_pairs={{0,64},{64,0},{1,65},{65,1},{2,66},{66,2},{3,67},{67,3},{4,68},{68... | collective-permute-start | bytes 49208 | tf_op jit(solution)/shard_map/ppermute | solution.py:80
  66.7 15.5 %collective-permute-start.8 = (bf16[3584,128]{1,0:T(8,128)(2,1)}, bf16[3584,128]{1,0:T(8,128)(2,1)}, u32[]{:S(2)}, u32[]{:S(2)}) collective-permute-start(bf16[3584,128]{1,0:T(8,128)(2,1)} %bitcast.148), channel_id=1, source_target_pairs={{0,32},{32,0},{1,33},{33,1},{2,34},{34,2},{3,35},{35,3},{4,36},{36... | collective-permute-start | bytes 2752520 | tf_op jit(solution)/shard_map/ppermute | solution.py:80
  75.9 12.4 %collective-permute-start.2 = (bf16[4096,112]{0,1:T(8,128)(2,1)S(1)}, bf16[4096,112]{0,1:T(8,128)(2,1)S(1)}, u32[]{:S(2)}, u32[]{:S(2)}) collective-permute-start(bf16[4096,112]{0,1:T(8,128)(2,1)S(1)} %bitcast.143), channel_id=1, source_target_pairs={{0,32},{32,0},{1,33},{33,1},{2,34},{34,2},{3,35},{35,3},{4,36},{36... | collective-permute-start | bytes 2752520 | tf_op jit(solution)/shard_map/ppermute | solution.py:80
  77.9 10.5 %collective-permute-start.6 = (bf16[4096,112]{0,1:T(8,128)(2,1)}, bf16[4096,112]{0,1:T(8,128)(2,1)S(1)}, u32[]{:S(2)}, u32[]{:S(2)}) collective-permute-start(bf16[4096,112]{0,1:T(8,128)(2,1)} %collective-permute-done.4), channel_id=1, source_target_pairs={{0,32},{32,0},{1,33},{33,1},{2,34},{34,2},{3,35},{35,3},{4,36},{36... | collective-permute-start | bytes 2752520 | tf_op jit(solution)/shard_map/ppermute | solution.py:80
  80.3 10.5 %collective-permute-start.7 = (bf16[4096,112]{0,1:T(8,128)(2,1)}, bf16[4096,112]{0,1:T(8,128)(2,1)}, u32[]{:S(2)}, u32[]{:S(2)}) collective-permute-start(bf16[4096,112]{0,1:T(8,128)(2,1)} %collective-permute-done.5), channel_id=1, source_target_pairs={{0,32},{32,0},{1,33},{33,1},{2,34},{34,2},{3,35},{35,3},{4,36},{36... | collective-permute-start | bytes 2752520 | tf_op jit(solution)/shard_map/ppermute | solution.py:80
  82.2 33.9 %collective-permute-start.18 = (bf16[3584,128]{1,0:T(8,128)(2,1)}, bf16[3584,128]{1,0:T(8,128)(2,1)}, u32[]{:S(2)}, u32[]{:S(2)}) collective-permute-start(bf16[3584,128]{1,0:T(8,128)(2,1)} %collective-permute-done.17), channel_id=1, source_target_pairs={{0,32},{32,0},{1,33},{33,1},{2,34},{34,2},{3,35},{35,3},{4,36},{36... | collective-permute-start | bytes 2752520 | tf_op jit(solution)/shard_map/ppermute | solution.py:80
  100.1 36.7 %copy-start.3 = (bf16[3584,256]{1,0:T(8,128)(2,1)S(1)}, bf16[3584,256]{1,0:T(8,128)(2,1)}, u32[]{:S(2)}) copy-start(bf16[3584,256]{1,0:T(8,128)(2,1)} %copy-done.2) | copy-start | bytes 5505028
  100.1 18.3 %collective-permute-start.10 = (bf16[496,256]{1,0:T(8,128)(2,1)}, bf16[496,256]{1,0:T(8,128)(2,1)S(1)}, u32[]{:S(2)}, u32[]{:S(2)}) collective-permute-start(bf16[496,256]{1,0:T(8,128)(2,1)} %hidden.1), channel_id=1, source_target_pairs={{0,896},{32,160},{128,0},{160,288},{256,128},{288,416},{384,256},{... | collective-permute-start | bytes 761864 | tf_op jit(solution)/shard_map/ppermute | solution.py:305
  102.7 23.6 %collective-permute-start.9 = (bf16[496,256]{1,0:T(8,128)(2,1)}, bf16[496,256]{1,0:T(8,128)(2,1)S(1)}, u32[]{:S(2)}, u32[]{:S(2)}) collective-permute-start(bf16[496,256]{1,0:T(8,128)(2,1)} %hidden.1), channel_id=1, source_target_pairs={{0,128},{32,928},{128,256},{160,32},{256,384},{288,160},{384,512},... | collective-permute-start | bytes 761864 | tf_op jit(solution)/shard_map/ppermute | solution.py:305
  129.0 10.6 %collective-permute-start.12 = (bf16[496,256]{1,0:T(8,128)(2,1)S(1)}, bf16[496,256]{1,0:T(8,128)(2,1)S(1)}, u32[]{:S(2)}, u32[]{:S(2)}) collective-permute-start(bf16[496,256]{1,0:T(8,128)(2,1)S(1)} %collective-permute-done.10), channel_id=1, source_target_pairs={{0,896},{32,160},{128,0},{160,288},{256,128},{288,416},{384,256},{... | collective-permute-start | bytes 761864 | tf_op jit(solution)/shard_map/ppermute | solution.py:305
  130.9 13.6 %collective-permute-start.11 = (bf16[496,256]{1,0:T(8,128)(2,1)S(1)}, bf16[496,256]{1,0:T(8,128)(2,1)S(1)}, u32[]{:S(2)}, u32[]{:S(2)}) collective-permute-start(bf16[496,256]{1,0:T(8,128)(2,1)S(1)} %collective-permute-done.9), channel_id=1, source_target_pairs={{0,128},{32,928},{128,256},{160,32},{256,384},{288,160},{384,512},... | collective-permute-start | bytes 761864 | tf_op jit(solution)/shard_map/ppermute | solution.py:305
  139.6 11.7 %collective-permute-start.14 = (bf16[496,256]{1,0:T(8,128)(2,1)S(1)}, bf16[496,256]{1,0:T(8,128)(2,1)S(1)}, u32[]{:S(2)}, u32[]{:S(2)}) collective-permute-start(bf16[496,256]{1,0:T(8,128)(2,1)S(1)} %collective-permute-done.12), channel_id=1, source_target_pairs={{0,896},{32,160},{128,0},{160,288},{256,128},{288,416},{384,256},{... | collective-permute-start | bytes 761864 | tf_op jit(solution)/shard_map/ppermute | solution.py:305
  144.5 11.8 %collective-permute-start.13 = (bf16[496,256]{1,0:T(8,128)(2,1)S(1)}, bf16[496,256]{1,0:T(8,128)(2,1)S(1)}, u32[]{:S(2)}, u32[]{:S(2)}) collective-permute-start(bf16[496,256]{1,0:T(8,128)(2,1)S(1)} %collective-permute-done.11), channel_id=1, source_target_pairs={{0,128},{32,928},{128,256},{160,32},{256,384},{288,160},{384,512},... | collective-permute-start | bytes 761864 | tf_op jit(solution)/shard_map/ppermute | solution.py:305
  151.4 13.5 %collective-permute-start.16 = (bf16[256,256]{1,0:T(8,128)(2,1)S(1)}, bf16[256,256]{1,0:T(8,128)(2,1)S(1)}, u32[]{:S(2)}, u32[]{:S(2)}) collective-permute-start(bf16[256,256]{1,0:T(8,128)(2,1)S(1)} %slice.132), channel_id=1, source_target_pairs={{0,896},{32,160},{128,0},{160,288},{256,128},{288,416},{384,256},{... | collective-permute-start | bytes 393224 | tf_op jit(solution)/shard_map/ppermute | solution.py:305
  156.3 8.1 %collective-permute-start.15 = (bf16[240,256]{1,0:T(8,128)(2,1)S(1)}, bf16[240,256]{1,0:T(8,128)(2,1)S(1)}, u32[]{:S(2)}, u32[]{:S(2)}) collective-permute-start(bf16[240,256]{1,0:T(8,128)(2,1)S(1)} %slice.130), channel_id=1, source_target_pairs={{0,128},{32,928},{128,256},{160,32},{256,384},{288,160},{384,512},... | collective-permute-start | bytes 368648 | tf_op jit(solution)/shard_map/ppermute | solution.py:305
  167.6 43.0 %all-to-all-start.1 = ((f32[128,8,128]{2,1,0:T(8,128)}), f32[128,8,128]{2,1,0:T(8,128)S(1)}, u32[]{:S(2)}, u32[]{:S(2)}) async-start(f32[128,8,128]{2,1,0:T(8,128)} %bitcast.32), calls=%async_computation.1 | async-start | bytes 1048576 | tf_op jit(solution)/shard_map/all_to_all | solution.py:401
  (29 other events, 449.8 us)

commit v4 on v3

--- a/solution.py
+++ b/solution.py
@@ -224,10 +224,10 @@
 
 
 def hidden_kernel(part_ref, slots_ref, head_ref, *refs):
-    pieces, (out_ref, slots, weights, slots_sem, sems) = refs[:8], refs[8:]
+    pieces, (out_ref, weights, sems) = refs[:8], refs[8:]
     count = pieces[0].shape[0]
     head = head_ref.shape[0]
-    copies = [pltpu.make_async_copy(slots_ref, slots, slots_sem)]
+    copies = []
     for i, piece in enumerate(pieces):
         copies.append(
             pltpu.make_async_copy(piece, weights.at[pl.ds(i * count, count)], sems.at[i])
@@ -235,15 +235,14 @@
     for copy in copies:
         copy.start()
     out_ref[pl.ds(0, head), :] = head_ref[...]
-    copies[0].wait()
     part = part_ref[0]
     for first in range(0, 4, 2):
-        for copy in copies[1 + 2 * first : 1 + 2 * (first + 2)]:
+        for copy in copies[2 * first : 2 * (first + 2)]:
             copy.wait()
         sums = [
             lax.dot_general(
                 weights[pl.ds(2 * count * member, 2 * count), :],
-                slots[...],
+                slots_ref[...],
                 (((1,), (1,)), ((), ())),
                 preferred_element_type=jnp.float32,
             )
@@ -259,23 +258,27 @@
 def ring_message(arrived, head, gates, ups):
     count = gates[0].shape[1]
     slot_count, width = arrived.shape
-    pieces = [weight.T for pair in zip(gates, ups) for weight in pair]
+    pieces = [
+        pltpu.with_memory_space_constraint(weight.T, pltpu.HBM)
+        for pair in zip(gates, ups)
+        for weight in pair
+    ]
     part = (lax.axis_index("zl") * 2 + lax.axis_index("core")).astype(jnp.int32).reshape(1)
     anywhere = pl.BlockSpec(memory_space=pl.ANY)
+    inside = pl.BlockSpec(memory_space=pltpu.VMEM)
+    arrived = pltpu.with_memory_space_constraint(arrived, pltpu.VMEM)
     return pl.pallas_call(
         hidden_kernel,
         out_shape=jax.ShapeDtypeStruct((head.shape[0] + 4 * count, slot_count), jnp.bfloat16),
         in_specs=[
             pl.BlockSpec(memory_space=pltpu.SMEM),
-            anywhere,
-            pl.BlockSpec(memory_space=pltpu.VMEM),
+            inside,
+            inside,
             *[anywhere] * 8,
         ],
-        out_specs=pl.BlockSpec(memory_space=pltpu.VMEM),
+        out_specs=inside,
         scratch_shapes=[
-            pltpu.VMEM((slot_count, width), jnp.bfloat16),
             pltpu.VMEM((8 * count, width), jnp.bfloat16),
-            pltpu.SemaphoreType.DMA,
             pltpu.SemaphoreType.DMA((8,)),
         ],
         cost_estimate=pl.CostEstimate(
@@ -283,6 +286,7 @@
             bytes_accessed=2 * (8 * count + slot_count) * width,
             transcendentals=4 * count * slot_count,
         ),
+        compiler_params=pltpu.CompilerParams(vmem_limit_bytes=24 * 2**20),
         name="hidden",
     )(part, arrived, head, *pieces)
 

time: 213 us -> 207 us (0.972)
  matrix products: 11.4 us -> 8.45 us
  Pallas kernels: 10.9 us -> 8.15 us
    dot_general x18, matrix products: 7.76 us -> 4.81 us  [product(): lax.dot_general(shard, lax.dynamic_slice_in_dim(down, start, shard.shape[...]
    pallas_call x1, Pallas kernels: 7.9 us -> 5.05 us  [ring_message(): pl.pallas_call(hidden_kernel, out_shape=jax.ShapeDtypeStruct((head.shape[...]
    unnamed x76 -> x70, local copies, waits for them, and re-layouts: 9.97 us -> 8.66 us
  transfers between devices with their start and end apart: 21 -> 21, of which waited for: 7 -> 8; matrix products, arithmetic and copies ran while one was open for 14% -> 13% of each run, Pallas kernels for 5% -> 4%
where the time goes in v4:
time: 207 us; the launch traced here: 206 us
  starting transfers between devices  112 us (54%)
  waiting for transfers between devices  50.1 us (24%)
  local copies, waits for them, and re-layouts  16.5 us (8%)
  other arithmetic  8.99 us (4%)
  matrix products  8.45 us (4%)
  Pallas kernels  8.15 us (4%)
    ppermute x11, starting transfers between devices, swap(): return lax.ppermute(array, axis, SWAP)  43.5 us
    ppermute x8, starting transfers between devices, move(): return lax.ppermute(array, ('zh', 'core'), pairs(way))  40.4 us
    all_to_all x1, starting transfers between devices, layer(): lax.all_to_all(blocks, ('exp', 'zl', 'core'), split_axis=0, concat_axis=0...  24.2 us
    ppermute x11, waiting for transfers between devices, swap(): return lax.ppermute(array, axis, SWAP)  18.8 us
    ppermute x8, waiting for transfers between devices, move(): return lax.ppermute(array, ('zh', 'core'), pairs(way))  17.2 us
    all_to_all x1, waiting for transfers between devices, layer(): lax.all_to_all(blocks, ('exp', 'zl', 'core'), split_axis=0, concat_axis=0...  14.1 us
    unnamed x70, local copies, waits for them, and re-layouts  8.66 us
    pallas_call x1, Pallas kernels, ring_message(): pl.pallas_call(hidden_kernel, out_shape=jax.ShapeDtypeStruct((head.shape[...  5.05 us
  transfers between devices with their start and end apart: 21, of which 8 were waited for; matrix products, arithmetic and copies ran while one was open for 13% of the time, Pallas kernels for 4%

profile of v4, /device:TPU:1, one launch (start us, length us, event | category | flops | bytes accessed | tf_op | source)
XLA Modules:
  0.0 206.0 jit_solution(17597782768391255779)
XLA Ops:
  0.7 5.0 %collective-permute-start.4 = (bf16[4096,112]{0,1:T(8,128)(2,1)}, bf16[4096,112]{0,1:T(8,128)(2,1)}, u32[]{:S(2)}, u32[]{:S(2)}) collective-permute-start(bf16[4096,112]{0,1:T(8,128)(2,1)} %bitcast.141), channel_id=1, source_target_pairs={{0,64},{64,0},{1,65},{65,1},{2,66},{66,2},{3,67},{67,3},{4,68},{68... | collective-permute-start | bytes 2752520 | tf_op jit(solution)/shard_map/ppermute | solution.py:80
  5.6 3.1 %pack.1 = bf16[256,4096]{1,0:T(8,128)(2,1)} custom-call(s32[1]{0:T(128)} %bitcast.part_ref, s32[2,128]{1,0:T(2,128)} %bitcast.164, bf16[128,4096]{1,0:T(8,128)(2,1)} %tokens_ref.1), custom_call_target="tpu_custom_call" | custom-call | flops 268435456 | bytes 3145728 | tf_op jit(solution)/shard_map/pack/pallas_call | solution.py:205
  8.7 13.1 %collective-permute-start.3 = (bf16[4096,112]{0,1:T(8,128)(2,1)}, bf16[4096,112]{0,1:T(8,128)(2,1)}, u32[]{:S(2)}, u32[]{:S(2)}) collective-permute-start(bf16[4096,112]{0,1:T(8,128)(2,1)} %bitcast.4), channel_id=1, source_target_pairs={{0,32},{32,0},{1,33},{33,1},{2,34},{34,2},{3,35},{35,3},{4,36},{36... | collective-permute-start | bytes 2752520 | tf_op jit(solution)/shard_map/ppermute | solution.py:80
  21.9 3.6 %collective-permute-start.5 = (bf16[4096,112]{0,1:T(8,128)(2,1)}, bf16[4096,112]{0,1:T(8,128)(2,1)}, u32[]{:S(2)}, u32[]{:S(2)}) collective-permute-start(bf16[4096,112]{0,1:T(8,128)(2,1)} %bitcast.4), channel_id=1, source_target_pairs={{0,64},{64,0},{1,65},{65,1},{2,66},{66,2},{3,67},{67,3},{4,68},{68... | collective-permute-start | bytes 2752520 | tf_op jit(solution)/shard_map/ppermute | solution.py:80
  25.7 2.4 %reduce-window.14 = f32[4,2,2,128]{3,2,1,0:T(2,128)S(1)} reduce-window(f32[4,2,2,128]{3,2,1,0:T(2,128)S(1)} %reshape.371, f32[]{:T(128)} %constant.33.clone.1), window={size=1x1x1x128 pad=0_0x0_0x0_0x127_0}, to_apply=%region_0.0 | reduce-window | flops 260096 | bytes 16388 | tf_op jit(solution)/shard_map/reduce-window
  30.9 2.3 %collective-permute-start = (f32[4,1025]{1,0:T(4,128)S(1)}, f32[4,1025]{1,0:T(4,128)S(1)}, u32[]{:S(2)}, u32[]{:S(2)}) collective-permute-start(f32[4,1025]{1,0:T(4,128)S(1)} %pad_maximum_fusion.2), channel_id=1, source_target_pairs={{0,32},{32,0},{1,33},{33,1},{2,34},{34,2},{3,35},{35,3},{4,36},{36... | collective-permute-start | bytes 49208 | tf_op jit(solution)/shard_map/ppermute | solution.py:80
  33.2 4.0 %all-to-all-start = ((bf16[32,8,4096]{2,1,0:T(8,128)(2,1)}), bf16[32,8,4096]{2,1,0:T(8,128)(2,1)S(1)}, u32[]{:S(2)}, u32[]{:S(2)}) async-start(bf16[32,8,4096]{2,1,0:T(8,128)(2,1)} %bitcast.138), calls=%async_computation | async-start | bytes 4194304 | tf_op jit(solution)/shard_map/all_to_all | solution.py:378
  44.6 3.4 %collective-permute-start.1 = (f32[4,1025]{1,0:T(4,128)S(1)}, f32[4,1025]{1,0:T(4,128)}, u32[]{:S(2)}, u32[]{:S(2)}) collective-permute-start(f32[4,1025]{1,0:T(4,128)S(1)} %pad_maximum_fusion.3), channel_id=1, source_target_pairs={{0,64},{64,0},{1,65},{65,1},{2,66},{66,2},{3,67},{67,3},{4,68},{68... | collective-permute-start | bytes 49208 | tf_op jit(solution)/shard_map/ppermute | solution.py:80
  48.0 18.7 %collective-permute-done.1 = f32[4,1025]{1,0:T(4,128)} collective-permute-done((f32[4,1025]{1,0:T(4,128)S(1)}, f32[4,1025]{1,0:T(4,128)}, u32[]{:S(2)}, u32[]{:S(2)}) %collective-permute-start.1) | collective-permute-done | bytes 16432 | tf_op jit(solution)/shard_map/ppermute | solution.py:80
  66.8 5.4 %collective-permute-start.8 = (bf16[3584,128]{1,0:T(8,128)(2,1)}, bf16[3584,128]{1,0:T(8,128)(2,1)}, u32[]{:S(2)}, u32[]{:S(2)}) collective-permute-start(bf16[3584,128]{1,0:T(8,128)(2,1)} %bitcast.148), channel_id=1, source_target_pairs={{0,32},{32,0},{1,33},{33,1},{2,34},{34,2},{3,35},{35,3},{4,36},{36... | collective-permute-start | bytes 2752520 | tf_op jit(solution)/shard_map/ppermute | solution.py:80
  78.1 2.4 %collective-permute-start.6 = (bf16[4096,112]{0,1:T(8,128)(2,1)}, bf16[4096,112]{0,1:T(8,128)(2,1)S(1)}, u32[]{:S(2)}, u32[]{:S(2)}) collective-permute-start(bf16[4096,112]{0,1:T(8,128)(2,1)} %collective-permute-done.4), channel_id=1, source_target_pairs={{0,32},{32,0},{1,33},{33,1},{2,34},{34,2},{3,35},{35,3},{4,36},{36... | collective-permute-start | bytes 2752520 | tf_op jit(solution)/shard_map/ppermute | solution.py:80
  82.4 2.4 %collective-permute-start.18 = (bf16[3584,128]{1,0:T(8,128)(2,1)}, bf16[3584,128]{1,0:T(8,128)(2,1)}, u32[]{:S(2)}, u32[]{:S(2)}) collective-permute-start(bf16[3584,128]{1,0:T(8,128)(2,1)} %collective-permute-done.17), channel_id=1, source_target_pairs={{0,32},{32,0},{1,33},{33,1},{2,34},{34,2},{3,35},{35,3},{4,36},{36... | collective-permute-start | bytes 2752520 | tf_op jit(solution)/shard_map/ppermute | solution.py:80
  91.1 5.1 %hidden.1 = bf16[496,256]{1,0:T(8,128)(2,1)S(1)} custom-call(s32[1]{0:T(128)} %bitcast.part_ref, bf16[256,4096]{1,0:T(8,128)(2,1)S(1)} %bitcast.137, bf16[48,256]{1,0:T(8,128)(2,1)S(1)} %pad_maximum_fusion.1.head_ref, bf16[112,4096]{1,0:T(8,128)(2,1)} %bitcast.142, bf16[112,4096]{1,0:T(8,128)(2,1)} %bitcast.18.refs_1_, bf16[112,4096]{1,0:T(8,128)(2,1)} %bitcast.144, ...), custom_call_target="tpu_custom_call" | custom-call | flops 1879048192 | bytes 9437184 | tf_op jit(solution)/shard_map/hidden/pallas_call | solution.py:270
  96.1 2.7 %collective-permute-start.10 = (bf16[496,256]{1,0:T(8,128)(2,1)S(1)}, bf16[496,256]{1,0:T(8,128)(2,1)S(1)}, u32[]{:S(2)}, u32[]{:S(2)}) collective-permute-start(bf16[496,256]{1,0:T(8,128)(2,1)S(1)} %hidden.1), channel_id=1, source_target_pairs={{0,896},{32,160},{128,0},{160,288},{256,128},{288,416},{384,256},{... | collective-permute-start | bytes 761864 | tf_op jit(solution)/shard_map/ppermute | solution.py:309
  98.8 13.4 %collective-permute-start.9 = (bf16[496,256]{1,0:T(8,128)(2,1)S(1)}, bf16[496,256]{1,0:T(8,128)(2,1)S(1)}, u32[]{:S(2)}, u32[]{:S(2)}) collective-permute-start(bf16[496,256]{1,0:T(8,128)(2,1)S(1)} %hidden.1), channel_id=1, source_target_pairs={{0,128},{32,928},{128,256},{160,32},{256,384},{288,160},{384,512},... | collective-permute-start | bytes 761864 | tf_op jit(solution)/shard_map/ppermute | solution.py:309
  114.3 7.8 %collective-permute-done.9 = bf16[496,256]{1,0:T(8,128)(2,1)S(1)} collective-permute-done((bf16[496,256]{1,0:T(8,128)(2,1)S(1)}, bf16[496,256]{1,0:T(8,128)(2,1)S(1)}, u32[]{:S(2)}, u32[]{:S(2)}) %collective-permute-start.9) | collective-permute-done | bytes 253984 | tf_op jit(solution)/shard_map/ppermute | solution.py:309
  124.6 5.9 %collective-permute-start.11 = (bf16[496,256]{1,0:T(8,128)(2,1)S(1)}, bf16[496,256]{1,0:T(8,128)(2,1)S(1)}, u32[]{:S(2)}, u32[]{:S(2)}) collective-permute-start(bf16[496,256]{1,0:T(8,128)(2,1)S(1)} %collective-permute-done.9), channel_id=1, source_target_pairs={{0,128},{32,928},{128,256},{160,32},{256,384},{288,160},{384,512},... | collective-permute-start | bytes 761864 | tf_op jit(solution)/shard_map/ppermute | solution.py:309
  131.4 3.5 %collective-permute-done.12 = bf16[496,256]{1,0:T(8,128)(2,1)S(1)} collective-permute-done((bf16[496,256]{1,0:T(8,128)(2,1)S(1)}, bf16[496,256]{1,0:T(8,128)(2,1)S(1)}, u32[]{:S(2)}, u32[]{:S(2)}) %collective-permute-start.12) | collective-permute-done | bytes 253984 | tf_op jit(solution)/shard_map/ppermute | solution.py:309
  138.3 5.6 %collective-permute-start.13 = (bf16[496,256]{1,0:T(8,128)(2,1)S(1)}, bf16[496,256]{1,0:T(8,128)(2,1)S(1)}, u32[]{:S(2)}, u32[]{:S(2)}) collective-permute-start(bf16[496,256]{1,0:T(8,128)(2,1)S(1)} %collective-permute-done.11), channel_id=1, source_target_pairs={{0,128},{32,928},{128,256},{160,32},{256,384},{288,160},{384,512},... | collective-permute-start | bytes 761864 | tf_op jit(solution)/shard_map/ppermute | solution.py:309
  146.3 3.3 %collective-permute-start.16 = (bf16[256,256]{1,0:T(8,128)(2,1)S(1)}, bf16[256,256]{1,0:T(8,128)(2,1)S(1)}, u32[]{:S(2)}, u32[]{:S(2)}) collective-permute-start(bf16[256,256]{1,0:T(8,128)(2,1)S(1)} %slice.132), channel_id=1, source_target_pairs={{0,896},{32,160},{128,0},{160,288},{256,128},{288,416},{384,256},{... | collective-permute-start | bytes 393224 | tf_op jit(solution)/shard_map/ppermute | solution.py:309
  149.6 5.7 %collective-permute-start.15 = (bf16[240,256]{1,0:T(8,128)(2,1)S(1)}, bf16[240,256]{1,0:T(8,128)(2,1)S(1)}, u32[]{:S(2)}, u32[]{:S(2)}) collective-permute-start(bf16[240,256]{1,0:T(8,128)(2,1)S(1)} %slice.130), channel_id=1, source_target_pairs={{0,128},{32,928},{128,256},{160,32},{256,384},{288,160},{384,512},... | collective-permute-start | bytes 368648 | tf_op jit(solution)/shard_map/ppermute | solution.py:309
  155.9 2.8 %collective-permute-done.15 = bf16[240,256]{1,0:T(8,128)(2,1)S(1)} collective-permute-done((bf16[240,256]{1,0:T(8,128)(2,1)S(1)}, bf16[240,256]{1,0:T(8,128)(2,1)S(1)}, u32[]{:S(2)}, u32[]{:S(2)}) %collective-permute-start.15) | collective-permute-done | bytes 122912 | tf_op jit(solution)/shard_map/ppermute | solution.py:309
  161.8 24.2 %all-to-all-start.1 = ((f32[128,8,128]{2,1,0:T(8,128)}), f32[128,8,128]{2,1,0:T(8,128)S(1)}, u32[]{:S(2)}, u32[]{:S(2)}) async-start(f32[128,8,128]{2,1,0:T(8,128)} %bitcast.32), calls=%async_computation.1 | async-start | bytes 1048576 | tf_op jit(solution)/shard_map/all_to_all | solution.py:405
  190.8 14.1 %all-to-all-done.1 = f32[128,8,128]{2,1,0:T(8,128)S(1)} async-done(((f32[128,8,128]{2,1,0:T(8,128)}), f32[128,8,128]{2,1,0:T(8,128)S(1)}, u32[]{:S(2)}, u32[]{:S(2)}) %all-to-all-start.1) | async-done | bytes 524320 | tf_op jit(solution)/shard_map/all_to_all | solution.py:405
  (213 shorter events, 44.6 us)
Async XLA Ops:
  0.6 28.9 %copy-start.8 = (bf16[512,256]{1,0:T(8,128)(2,1)S(1)}, bf16[512,256]{1,0:T(8,128)(2,1)}, u32[]{:S(2)}) copy-start(bf16[512,256]{1,0:T(8,128)(2,1)} %param.15) | copy-start | bytes 786436
  0.7 75.4 %collective-permute-start.4 = (bf16[4096,112]{0,1:T(8,128)(2,1)}, bf16[4096,112]{0,1:T(8,128)(2,1)}, u32[]{:S(2)}, u32[]{:S(2)}) collective-permute-start(bf16[4096,112]{0,1:T(8,128)(2,1)} %bitcast.141), channel_id=1, source_target_pairs={{0,64},{64,0},{1,65},{65,1},{2,66},{66,2},{3,67},{67,3},{4,68},{68... | collective-permute-start | bytes 2752520 | tf_op jit(solution)/shard_map/ppermute | solution.py:80
  8.7 79.8 %collective-permute-start.3 = (bf16[4096,112]{0,1:T(8,128)(2,1)}, bf16[4096,112]{0,1:T(8,128)(2,1)}, u32[]{:S(2)}, u32[]{:S(2)}) collective-permute-start(bf16[4096,112]{0,1:T(8,128)(2,1)} %bitcast.4), channel_id=1, source_target_pairs={{0,32},{32,0},{1,33},{33,1},{2,34},{34,2},{3,35},{35,3},{4,36},{36... | collective-permute-start | bytes 2752520 | tf_op jit(solution)/shard_map/ppermute | solution.py:80
  21.9 56.2 %collective-permute-start.5 = (bf16[4096,112]{0,1:T(8,128)(2,1)}, bf16[4096,112]{0,1:T(8,128)(2,1)}, u32[]{:S(2)}, u32[]{:S(2)}) collective-permute-start(bf16[4096,112]{0,1:T(8,128)(2,1)} %bitcast.4), channel_id=1, source_target_pairs={{0,64},{64,0},{1,65},{65,1},{2,66},{66,2},{3,67},{67,3},{4,68},{68... | collective-permute-start | bytes 2752520 | tf_op jit(solution)/shard_map/ppermute | solution.py:80
  30.9 13.1 %collective-permute-start = (f32[4,1025]{1,0:T(4,128)S(1)}, f32[4,1025]{1,0:T(4,128)S(1)}, u32[]{:S(2)}, u32[]{:S(2)}) collective-permute-start(f32[4,1025]{1,0:T(4,128)S(1)} %pad_maximum_fusion.2), channel_id=1, source_target_pairs={{0,32},{32,0},{1,33},{33,1},{2,34},{34,2},{3,35},{35,3},{4,36},{36... | collective-permute-start | bytes 49208 | tf_op jit(solution)/shard_map/ppermute | solution.py:80
  33.2 57.8 %all-to-all-start = ((bf16[32,8,4096]{2,1,0:T(8,128)(2,1)}), bf16[32,8,4096]{2,1,0:T(8,128)(2,1)S(1)}, u32[]{:S(2)}, u32[]{:S(2)}) async-start(bf16[32,8,4096]{2,1,0:T(8,128)(2,1)} %bitcast.138), calls=%async_computation | async-start | bytes 4194304 | tf_op jit(solution)/shard_map/all_to_all | solution.py:378
  37.2 38.9 %copy-start.4 = (bf16[1,4096,112]{1,2,0:T(8,128)(2,1)S(1)}, bf16[1,4096,112]{1,2,0:T(8,128)(2,1)}, u32[]{:S(2)}) copy-start(bf16[1,4096,112]{1,2,0:T(8,128)(2,1)} %param.24) | copy-start | bytes 2752516
  37.2 43.2 %collective-permute-start.17 = (bf16[3584,128]{1,0:T(8,128)(2,1)}, bf16[3584,128]{1,0:T(8,128)(2,1)}, u32[]{:S(2)}, u32[]{:S(2)}) collective-permute-start(bf16[3584,128]{1,0:T(8,128)(2,1)} %bitcast.146), channel_id=1, source_target_pairs={{0,64},{64,0},{1,65},{65,1},{2,66},{66,2},{3,67},{67,3},{4,68},{68... | collective-permute-start | bytes 2752520 | tf_op jit(solution)/shard_map/ppermute | solution.py:80
  44.6 22.2 %collective-permute-start.1 = (f32[4,1025]{1,0:T(4,128)S(1)}, f32[4,1025]{1,0:T(4,128)}, u32[]{:S(2)}, u32[]{:S(2)}) collective-permute-start(f32[4,1025]{1,0:T(4,128)S(1)} %pad_maximum_fusion.3), channel_id=1, source_target_pairs={{0,64},{64,0},{1,65},{65,1},{2,66},{66,2},{3,67},{67,3},{4,68},{68... | collective-permute-start | bytes 49208 | tf_op jit(solution)/shard_map/ppermute | solution.py:80
  66.8 15.6 %collective-permute-start.8 = (bf16[3584,128]{1,0:T(8,128)(2,1)}, bf16[3584,128]{1,0:T(8,128)(2,1)}, u32[]{:S(2)}, u32[]{:S(2)}) collective-permute-start(bf16[3584,128]{1,0:T(8,128)(2,1)} %bitcast.148), channel_id=1, source_target_pairs={{0,32},{32,0},{1,33},{33,1},{2,34},{34,2},{3,35},{35,3},{4,36},{36... | collective-permute-start | bytes 2752520 | tf_op jit(solution)/shard_map/ppermute | solution.py:80
  76.1 12.4 %collective-permute-start.2 = (bf16[4096,112]{0,1:T(8,128)(2,1)S(1)}, bf16[4096,112]{0,1:T(8,128)(2,1)S(1)}, u32[]{:S(2)}, u32[]{:S(2)}) collective-permute-start(bf16[4096,112]{0,1:T(8,128)(2,1)S(1)} %bitcast.143), channel_id=1, source_target_pairs={{0,32},{32,0},{1,33},{33,1},{2,34},{34,2},{3,35},{35,3},{4,36},{36... | collective-permute-start | bytes 2752520 | tf_op jit(solution)/shard_map/ppermute | solution.py:80
  78.1 10.5 %collective-permute-start.6 = (bf16[4096,112]{0,1:T(8,128)(2,1)}, bf16[4096,112]{0,1:T(8,128)(2,1)S(1)}, u32[]{:S(2)}, u32[]{:S(2)}) collective-permute-start(bf16[4096,112]{0,1:T(8,128)(2,1)} %collective-permute-done.4), channel_id=1, source_target_pairs={{0,32},{32,0},{1,33},{33,1},{2,34},{34,2},{3,35},{35,3},{4,36},{36... | collective-permute-start | bytes 2752520 | tf_op jit(solution)/shard_map/ppermute | solution.py:80
  80.5 10.6 %collective-permute-start.7 = (bf16[4096,112]{0,1:T(8,128)(2,1)}, bf16[4096,112]{0,1:T(8,128)(2,1)}, u32[]{:S(2)}, u32[]{:S(2)}) collective-permute-start(bf16[4096,112]{0,1:T(8,128)(2,1)} %collective-permute-done.5), channel_id=1, source_target_pairs={{0,32},{32,0},{1,33},{33,1},{2,34},{34,2},{3,35},{35,3},{4,36},{36... | collective-permute-start | bytes 2752520 | tf_op jit(solution)/shard_map/ppermute | solution.py:80
  82.4 29.8 %collective-permute-start.18 = (bf16[3584,128]{1,0:T(8,128)(2,1)}, bf16[3584,128]{1,0:T(8,128)(2,1)}, u32[]{:S(2)}, u32[]{:S(2)}) collective-permute-start(bf16[3584,128]{1,0:T(8,128)(2,1)} %collective-permute-done.17), channel_id=1, source_target_pairs={{0,32},{32,0},{1,33},{33,1},{2,34},{34,2},{3,35},{35,3},{4,36},{36... | collective-permute-start | bytes 2752520 | tf_op jit(solution)/shard_map/ppermute | solution.py:80
  96.1 34.4 %copy-start.2 = (bf16[3584,256]{1,0:T(8,128)(2,1)S(1)}, bf16[3584,256]{1,0:T(8,128)(2,1)}, u32[]{:S(2)}) copy-start(bf16[3584,256]{1,0:T(8,128)(2,1)} %copy-done.1) | copy-start | bytes 5505028
  96.1 17.9 %collective-permute-start.10 = (bf16[496,256]{1,0:T(8,128)(2,1)S(1)}, bf16[496,256]{1,0:T(8,128)(2,1)S(1)}, u32[]{:S(2)}, u32[]{:S(2)}) collective-permute-start(bf16[496,256]{1,0:T(8,128)(2,1)S(1)} %hidden.1), channel_id=1, source_target_pairs={{0,896},{32,160},{128,0},{160,288},{256,128},{288,416},{384,256},{... | collective-permute-start | bytes 761864 | tf_op jit(solution)/shard_map/ppermute | solution.py:309
  98.8 23.3 %collective-permute-start.9 = (bf16[496,256]{1,0:T(8,128)(2,1)S(1)}, bf16[496,256]{1,0:T(8,128)(2,1)S(1)}, u32[]{:S(2)}, u32[]{:S(2)}) collective-permute-start(bf16[496,256]{1,0:T(8,128)(2,1)S(1)} %hidden.1), channel_id=1, source_target_pairs={{0,128},{32,928},{128,256},{160,32},{256,384},{288,160},{384,512},... | collective-permute-start | bytes 761864 | tf_op jit(solution)/shard_map/ppermute | solution.py:309
  122.7 12.2 %collective-permute-start.12 = (bf16[496,256]{1,0:T(8,128)(2,1)S(1)}, bf16[496,256]{1,0:T(8,128)(2,1)S(1)}, u32[]{:S(2)}, u32[]{:S(2)}) collective-permute-start(bf16[496,256]{1,0:T(8,128)(2,1)S(1)} %collective-permute-done.10), channel_id=1, source_target_pairs={{0,896},{32,160},{128,0},{160,288},{256,128},{288,416},{384,256},{... | collective-permute-start | bytes 761864 | tf_op jit(solution)/shard_map/ppermute | solution.py:309
  124.6 13.6 %collective-permute-start.11 = (bf16[496,256]{1,0:T(8,128)(2,1)S(1)}, bf16[496,256]{1,0:T(8,128)(2,1)S(1)}, u32[]{:S(2)}, u32[]{:S(2)}) collective-permute-start(bf16[496,256]{1,0:T(8,128)(2,1)S(1)} %collective-permute-done.9), channel_id=1, source_target_pairs={{0,128},{32,928},{128,256},{160,32},{256,384},{288,160},{384,512},... | collective-permute-start | bytes 761864 | tf_op jit(solution)/shard_map/ppermute | solution.py:309
  134.9 11.4 %collective-permute-start.14 = (bf16[496,256]{1,0:T(8,128)(2,1)S(1)}, bf16[496,256]{1,0:T(8,128)(2,1)S(1)}, u32[]{:S(2)}, u32[]{:S(2)}) collective-permute-start(bf16[496,256]{1,0:T(8,128)(2,1)S(1)} %collective-permute-done.12), channel_id=1, source_target_pairs={{0,896},{32,160},{128,0},{160,288},{256,128},{288,416},{384,256},{... | collective-permute-start | bytes 761864 | tf_op jit(solution)/shard_map/ppermute | solution.py:309
  138.3 11.3 %collective-permute-start.13 = (bf16[496,256]{1,0:T(8,128)(2,1)S(1)}, bf16[496,256]{1,0:T(8,128)(2,1)S(1)}, u32[]{:S(2)}, u32[]{:S(2)}) collective-permute-start(bf16[496,256]{1,0:T(8,128)(2,1)S(1)} %collective-permute-done.11), channel_id=1, source_target_pairs={{0,128},{32,928},{128,256},{160,32},{256,384},{288,160},{384,512},... | collective-permute-start | bytes 761864 | tf_op jit(solution)/shard_map/ppermute | solution.py:309
  146.3 12.8 %collective-permute-start.16 = (bf16[256,256]{1,0:T(8,128)(2,1)S(1)}, bf16[256,256]{1,0:T(8,128)(2,1)S(1)}, u32[]{:S(2)}, u32[]{:S(2)}) collective-permute-start(bf16[256,256]{1,0:T(8,128)(2,1)S(1)} %slice.132), channel_id=1, source_target_pairs={{0,896},{32,160},{128,0},{160,288},{256,128},{288,416},{384,256},{... | collective-permute-start | bytes 393224 | tf_op jit(solution)/shard_map/ppermute | solution.py:309
  149.6 9.1 %collective-permute-start.15 = (bf16[240,256]{1,0:T(8,128)(2,1)S(1)}, bf16[240,256]{1,0:T(8,128)(2,1)S(1)}, u32[]{:S(2)}, u32[]{:S(2)}) collective-permute-start(bf16[240,256]{1,0:T(8,128)(2,1)S(1)} %slice.130), channel_id=1, source_target_pairs={{0,128},{32,928},{128,256},{160,32},{256,384},{288,160},{384,512},... | collective-permute-start | bytes 368648 | tf_op jit(solution)/shard_map/ppermute | solution.py:309
  161.8 43.1 %all-to-all-start.1 = ((f32[128,8,128]{2,1,0:T(8,128)}), f32[128,8,128]{2,1,0:T(8,128)S(1)}, u32[]{:S(2)}, u32[]{:S(2)}) async-start(f32[128,8,128]{2,1,0:T(8,128)} %bitcast.32), calls=%async_computation.1 | async-start | bytes 1048576 | tf_op jit(solution)/shard_map/all_to_all | solution.py:405
  (26 other events, 415.1 us)
